TPU v7x, 32 devices: a whole 2x2x4 slice. The times are simulated.
32 devices in a mesh: rep: 1, r: 8 (over y, z), s: 4 (over x, core).
Axes of the slice: x: 2, y: 2, z: 4, core: 2. Of those that a mesh axis runs over, the one named last changes fastest.
Arguments:
- x: bfloat16 [32, 4096, 512], P(('rep', 'r', 's'))
- dy: bfloat16 [32, 4096, 512], P(('rep', 'r', 's'))
- w_gate: bfloat16 [2, 512, 1280], P(None, 's')
- w_up: bfloat16 [2, 512, 1280], P(None, 's')
- w_down: bfloat16 [2, 1280, 512], P(None, 's')
- m_w_gate: float32 [2, 512, 1280], P(None, 's')
- m_w_up: float32 [2, 512, 1280], P(None, 's')
- m_w_down: float32 [2, 1280, 512], P(None, 's')
- v_w_gate: float32 [2, 512, 1280], P(None, 's')
- v_w_up: float32 [2, 512, 1280], P(None, 's')
- v_w_down: float32 [2, 1280, 512], P(None, 's')
Outputs:
- output 1: bfloat16 [2, 512, 1280], P('rep', 's')
- output 2: bfloat16 [2, 512, 1280], P('rep', 's')
- output 3: bfloat16 [2, 1280, 512], P('rep', 's')
- output 4: float32 [2, 512, 1280], P('rep', 's')
- output 5: float32 [2, 512, 1280], P('rep', 's')
- output 6: float32 [2, 1280, 512], P('rep', 's')
- output 7: float32 [2, 512, 1280], P('rep', 's')
- output 8: float32 [2, 512, 1280], P('rep', 's')
- output 9: float32 [2, 1280, 512], P('rep', 's')
All inputs are finite; a program needn't handle non-finite values.
Results may differ from a plain program's by a relative error of at most 0.022.
Values are sent between devices in bfloat16 or wider.
A program may use at most 2 GiB of HBM per device.

v0:
```python
import jax
import jax.numpy as jnp
from jax import lax
from jax.sharding import PartitionSpec as P

NAMES = ("w_gate", "w_up", "w_down")


def matmul(a, w):
    return jnp.dot(a, w, preferred_element_type=jnp.float32).astype(jnp.bfloat16)


def normed(h):
    wide = h.astype(jnp.float32)
    scale = lax.rsqrt(jnp.mean(wide**2, -1, keepdims=True) + 1e-6)
    return (wide * scale).astype(jnp.bfloat16)


def layer(h, w):
    a = normed(h)
    gate = jnp.dot(a, w["w_gate"], preferred_element_type=jnp.float32)
    up = jnp.dot(a, w["w_up"], preferred_element_type=jnp.float32)
    return h + matmul((jax.nn.silu(gate) * up).astype(jnp.bfloat16), w["w_down"])


def adamw(w, m, v, g):
    m = 0.9 * m + 0.1 * g
    v = 0.95 * v + 0.05 * g * g
    step = m * lax.rsqrt(v + 1e-8) + 0.1 * w
    return (w - 0.02 * step).astype(jnp.bfloat16), m, v


def clipped(gradients, sum_of_squares, count):
    factor = jnp.minimum(1.0, 0.5 * lax.rsqrt(sum_of_squares / count + 1e-30))
    return [g * factor for g in gradients]


def solution(mesh):
    def fetched(weights, number):
        return {name: lax.all_gather(w[number], "s", axis=0, tiled=True) for name, w in zip(NAMES, weights, strict=True)}

    def summed(term):
        return lax.psum(lax.psum_scatter(term, "s", scatter_dimension=0, tiled=True), "r")

    def step(x, dy, *arrays):
        weights, m, v = (arrays[i : i + 3] for i in (0, 3, 6))
        layers = weights[0].shape[0]
        h, kept = x[0], []
        for number in range(layers):
            kept.append(h)
            h = layer(h, fetched(weights, number))
        by_h, mine = dy[0], [None] * layers
        for number in reversed(range(layers)):
            _, back = jax.vjp(lambda w, h: layer(h, w), fetched(weights, number), kept[number])
            by_w, by_h = back(by_h)
            mine[number] = [summed(by_w[name]) for name in NAMES]
        gradients = [jnp.stack([mine[number][i] for number in range(layers)]).astype(jnp.float32) for i in range(3)]
        squares = lax.psum(sum(jnp.sum(g * g) for g in gradients), "s")
        gradients = clipped(gradients, squares, lax.psum(1, "s") * sum(g.size for g in gradients))
        new = [adamw(w.astype(jnp.float32), m, v, g) for w, m, v, g in zip(weights, m, v, gradients, strict=True)]
        return tuple(one[which] for which in range(3) for one in new)

    states, cut = P(("rep", "r", "s"), None, None), P(None, "s", None)
    return jax.shard_map(
        step,
        mesh=mesh,
        in_specs=(states, states) + (cut,) * 9,
        out_specs=(P("rep", "s", None),) * 9,
        check_vma=False,
    )
```

profile of v0, /device:TPU:0, one launch (start us, length us, event | category | flops | bytes accessed | tf_op | source)
XLA Modules:
  0.0 506.1 jit_solution(17517882399926751519)
XLA Ops:
  15.0 6.5 %copy.20 = bf16[1,4096,512]{1,2,0:T(8,128)(2,1)} copy(bf16[1,4096,512]{2,1,0:T(8,128)(2,1)} %param.11) | data formatting | bytes 8388608 | tf_op args[0]
  21.5 3.1 fusion.15
  24.6 6.5 %copy.21 = bf16[1,4096,512]{1,2,0:T(8,128)(2,1)} copy(bf16[1,4096,512]{2,1,0:T(8,128)(2,1)} %param.12) | data formatting | bytes 8388608 | tf_op args[1]
  31.1 11.9 %fusion.47 = f32[4096,1280]{1,0:T(8,128)} fusion(bf16[1,4096,512]{1,2,0:T(8,128)(2,1)} %copy.20, f32[4096]{0:T(1024)S(1)} %add_rsqrt_fusion, bf16[1,512,1280]{2,1,0:T(8,128)(2,1)} %all-gather.13.cloned.1.call-done), kind=kOutput, calls=%fused_computation.57 | convolution fusion | flops 5375000576 | bytes 26492928 | tf_op jit(solution)/shard_map/dot_general | solution.py:21
  43.0 8.0 %all-gather.15.cloned.1.call-done = bf16[1,512,1280]{2,1,0:T(8,128)(2,1)} async-done(((bf16[1,128,1280]{2,1,0:T(8,128)(2,1)}), bf16[1,512,1280]{2,1,0:T(8,128)(2,1)}) %all-gather.15.cloned.1.call-update) | async-done | bytes 1310736 | tf_op jit(solution)/shard_map/all_gather | solution.py:40
  51.0 19.1 %multiply_convert_fusion.1 = (bf16[4096,1280]{1,0:T(8,128)(2,1)}, f32[4096,1280]{1,0:T(8,128)}) fusion(f32[4096,1280]{1,0:T(8,128)} %fusion.47, bf16[1,512,1280]{2,1,0:T(8,128)(2,1)} %all-gather.15.cloned.1.call-done, bf16[1,4096,512]{1,2,0:T(8,128)(2,1)} %copy.20, f32[4096]{0:T(1024)S(1)} %add_rsqrt_fusion), kind=kOutput, calls=%fused_computation.17 | convolution fusion | flops 5406457856 | bytes 57950208 | tf_op jit(solution)/shard_map/dot_general | solution.py:22
  71.1 11.4 %fusion.19 = (f32[4096]{0:T(1024)S(1)}, bf16[4096,512]{0,1:T(8,128)(2,1)}) fusion(bf16[4096,1280]{1,0:T(8,128)(2,1)} %get-tuple-element.30, bf16[1,1280,512]{2,1,0:T(8,128)(2,1)} %all-gather.17.cloned.1.call-done, bf16[1,4096,512]{1,2,0:T(8,128)(2,1)} %copy.20), kind=kOutput, calls=%fused_computation.37 | convolution fusion | flops 5379190784 | bytes 20201472 | tf_op jit(solution)/shard_map/dot_general | solution.py:10
  82.5 8.6 %all-gather.21.cloned.1.call-done = bf16[1,1280,512]{2,1,0:T(8,128)(2,1)} async-done(((bf16[1,320,512]{2,1,0:T(8,128)(2,1)}), bf16[1,1280,512]{2,1,0:T(8,128)(2,1)}) %all-gather.21.cloned.1.call-update) | async-done | bytes 1310736 | tf_op jit(solution)/shard_map/all_gather | solution.py:40
  91.1 10.5 %convolution_convert_fusion.1 = bf16[4096,1280]{1,0:T(8,128)(2,1)} fusion(bf16[1,4096,512]{2,1,0:T(8,128)(2,1)} %param.12, bf16[1,1280,512]{2,1,0:T(8,128)(2,1)} %all-gather.21.cloned.1.call-done), kind=kOutput, calls=%fused_computation.21 | convolution fusion | flops 5373952000 | bytes 15990784 | tf_op jit(solution)/shard_map/transpose(jvp())/dot_general | solution.py:10
  101.6 9.4 %all-gather.23.cloned.1.call-done = bf16[1,512,1280]{2,1,0:T(8,128)(2,1)} async-done(((bf16[1,128,1280]{2,1,0:T(8,128)(2,1)}), bf16[1,512,1280]{2,1,0:T(8,128)(2,1)}) %all-gather.23.cloned.1.call-update) | async-done | bytes 1310736 | tf_op jit(solution)/shard_map/all_gather | solution.py:40
  111.1 11.9 %fusion.39 = f32[4096,1280]{1,0:T(8,128)} fusion(bf16[4096,512]{0,1:T(8,128)(2,1)} %get-tuple-element.33, f32[4096]{0:T(1024)S(1)} %fusion.79, bf16[1,512,1280]{2,1,0:T(8,128)(2,1)} %all-gather.23.cloned.1.call-done), kind=kOutput, calls=%fused_computation.54 | convolution fusion | flops 5375000576 | bytes 26492928 | tf_op jit(solution)/shard_map/jvp()/dot_general | solution.py:22
  123.0 8.1 %all-gather.19.cloned.1.call-done = bf16[1,512,1280]{2,1,0:T(8,128)(2,1)} async-done(((bf16[1,128,1280]{2,1,0:T(8,128)(2,1)}), bf16[1,512,1280]{2,1,0:T(8,128)(2,1)}) %all-gather.19.cloned.1.call-update) | async-done | bytes 1310736 | tf_op jit(solution)/shard_map/all_gather | solution.py:40
  131.0 28.9 %fusion.2 = (bf16[4096,1280]{1,0:T(8,128)(2,1)}, f32[4096,1280]{1,0:T(8,128)}) fusion(f32[4096,1280]{1,0:T(8,128)} %fusion.39, bf16[4096,1280]{1,0:T(8,128)(2,1)} %convolution_convert_fusion.1, bf16[1,512,1280]{2,1,0:T(8,128)(2,1)} %all-gather.19.cloned.1.call-done, bf16[4096,512]{0,1:T(8,128)(2,1)} %get-tuple-element.33, f32[4096]{0:T(1024)S(1)} %fusion.79), kind=kOutput, calls=%fused_computation.8 | convolution fusion | flops 5437915136 | bytes 68435968 | tf_op jit(solution)/shard_map/jvp()/dot_general | solution.py:21
  159.9 9.6 %convolution_convert_fusion.4 = bf16[512,1280]{1,0:T(8,128)(2,1)} fusion(bf16[4096,1280]{1,0:T(8,128)(2,1)} %get-tuple-element.34, bf16[4096,512]{0,1:T(8,128)(2,1)S(1)} %copy-done.2, f32[4096]{0:T(1024)S(1)} %fusion.79), kind=kOutput, calls=%fused_computation.51 | convolution fusion | flops 5375000576 | bytes 16007168 | tf_op jit(solution)/shard_map/transpose(jvp())/dot_general | solution.py:21
  169.6 15.5 %fusion.22 = bf16[4096,512]{0,1:T(8,128)(2,1)} fusion(bf16[4096,1280]{1,0:T(8,128)(2,1)} %convolution_convert_fusion.1, bf16[1,512,1280]{2,1,0:T(8,128)(2,1)S(1)} %copy-done.20, f32[4096,1280]{1,0:T(8,128)} %get-tuple-element.35), kind=kOutput, calls=%fused_computation.41 | convolution fusion | flops 5402263552 | bytes 36962304 | tf_op jit(solution)/shard_map/transpose(jvp())/dot_general | solution.py:22
  185.2 11.1 %fusion.21 = (f32[4096]{0:T(1024)S(1)}, bf16[4096,512]{0,1:T(8,128)(2,1)S(1)}) fusion(bf16[4096,512]{0,1:T(8,128)(2,1)S(1)} %copy-done.3, bf16[4096,512]{0,1:T(8,128)(2,1)} %fusion.22, bf16[4096,1280]{1,0:T(8,128)(2,1)} %get-tuple-element.34, bf16[1,512,1280]{2,1,0:T(8,128)(2,1)S(1)} %copy-done.21), kind=kOutput, calls=%fused_computation.39 | convolution fusion | flops 5379190784 | bytes 24395776 | tf_op jit(solution)/shard_map/transpose(jvp())/dot_general | solution.py:21
  196.3 2.8 fusion.25
  199.2 8.3 %convolution_convert_fusion = bf16[4096,1280]{1,0:T(8,128)(2,1)} fusion(bf16[4096,512]{0,1:T(8,128)(2,1)S(1)} %fusion.25, bf16[1,1280,512]{2,1,0:T(8,128)(2,1)S(1)} %copy-done.19), kind=kOutput, calls=%fused_computation.20 | convolution fusion | flops 5373952000 | bytes 15990784 | tf_op jit(solution)/shard_map/transpose(jvp())/dot_general | solution.py:10
  207.6 20.6 %fusion.32 = bf16[512,1280]{1,0:T(8,128)(2,1)} fusion(f32[4096,1280]{1,0:T(8,128)} %fusion.47, f32[4096,1280]{1,0:T(8,128)} %get-tuple-element.31, bf16[4096,1280]{1,0:T(8,128)(2,1)} %convolution_convert_fusion, bf16[1,4096,512]{1,2,0:T(8,128)(2,1)S(1)} %copy-done, f32[4096]{0:T(1024)S(1)} %copy-done.18), kind=kOutput, calls=%fused_computation.49 | convolution fusion | flops 5433327616 | bytes 57950208 | tf_op jit(solution)/shard_map/transpose(jvp())/dot_general | solution.py:21
  228.3 16.3 %fusion.36 = bf16[512,1280]{1,0:T(8,128)(2,1)} fusion(bf16[4096,1280]{1,0:T(8,128)(2,1)} %convolution_convert_fusion.1, bf16[4096,512]{0,1:T(8,128)(2,1)} %get-tuple-element.33, f32[4096]{0:T(1024)S(1)} %fusion.79, f32[4096,1280]{1,0:T(8,128)} %get-tuple-element.35), kind=kOutput, calls=%fused_computation.52 | convolution fusion | flops 5407113216 | bytes 36978688 | tf_op jit(solution)/shard_map/transpose(jvp())/dot_general | solution.py:22
  244.6 16.3 %fusion.35 = bf16[512,1280]{1,0:T(8,128)(2,1)} fusion(bf16[4096,1280]{1,0:T(8,128)(2,1)} %convolution_convert_fusion, f32[4096,1280]{1,0:T(8,128)} %fusion.47, bf16[1,4096,512]{1,2,0:T(8,128)(2,1)} %copy.20, f32[4096]{0:T(1024)S(1)} %copy-done.18), kind=kOutput, calls=%fused_computation.50 | convolution fusion | flops 5407113216 | bytes 36978688 | tf_op jit(solution)/shard_map/transpose(jvp())/dot_general | solution.py:22
  261.0 18.4 %fusion.29 = bf16[1280,512]{1,0:T(8,128)(2,1)} fusion(bf16[1,4096,512]{2,1,0:T(8,128)(2,1)} %param.12, f32[4096,1280]{1,0:T(8,128)} %fusion.39, f32[4096,1280]{1,0:T(8,128)} %get-tuple-element.35), kind=kOutput, calls=%fused_computation.48 | convolution fusion | flops 5400821760 | bytes 47448064 | tf_op jit(solution)/shard_map/transpose(jvp())/dot_general | solution.py:10
  279.4 10.5 %convolution_convert_fusion.5 = bf16[1280,512]{1,0:T(8,128)(2,1)} fusion(bf16[4096,1280]{1,0:T(8,128)(2,1)} %get-tuple-element.30, bf16[4096,512]{0,1:T(8,128)(2,1)} %copy-done.4), kind=kOutput, calls=%fused_computation.53 | convolution fusion | flops 5369364480 | bytes 15990784 | tf_op jit(solution)/shard_map/transpose(jvp())/dot_general | solution.py:10
  290.1 23.4 %reduce-scatter.11.cloned.1.call-done = bf16[128,1280]{1,0:T(8,128)(2,1)} async-done(((bf16[512,1280]{1,0:T(8,128)(2,1)}), bf16[128,1280]{1,0:T(8,128)(2,1)}) %reduce-scatter.11.cloned.1.call-update) | async-done | bytes 327696 | tf_op jit(solution)/shard_map/reduce_scatter | solution.py:43
  313.4 29.4 %reduce-scatter.17.cloned.1.call-done = bf16[320,512]{1,0:T(8,128)(2,1)} async-done(((bf16[1280,512]{1,0:T(8,128)(2,1)}), bf16[320,512]{1,0:T(8,128)(2,1)}) %reduce-scatter.17.cloned.1.call-update) | async-done | bytes 327696 | tf_op jit(solution)/shard_map/reduce_scatter | solution.py:43
  342.9 29.3 %reduce-scatter.15.cloned.1.call-done = bf16[320,512]{1,0:T(8,128)(2,1)} async-done(((bf16[1280,512]{1,0:T(8,128)(2,1)}), bf16[320,512]{1,0:T(8,128)(2,1)}) %reduce-scatter.15.cloned.1.call-update) | async-done | bytes 327696 | tf_op jit(solution)/shard_map/reduce_scatter | solution.py:43
  372.2 103.2 %all-reduce.3.cloned.1.call-done = (bf16[1,128,1280]{2,1,0:T(8,128)(2,1)}, bf16[1,128,1280]{2,1,0:T(8,128)(2,1)}, bf16[1,128,1280]{2,1,0:T(8,128)(2,1)}, bf16[1,...) async-done(((bf16[1,128,1280]{2,1,0:T(8,128)(2,1)}, bf16[1,128,1280]{2,1,0:T(8,128)(2,1)}, bf16[1,128,1280]{2,1,0:T(8,128)(2,1)}, ...) | async-done | bytes 1966096 | tf_op jit(solution)/shard_map/psum | solution.py:43
  477.4 2.1 fusion.59
  480.8 2.0 fusion.60
  483.5 6.9 %psum.55 = f32[]{:T(128)} all-reduce(f32[]{:T(128)S(6)} %add.111), channel_id=1, replica_groups=mesh['rep'=1,'r'=8,'s'=4] {'s'}, use_global_device_ids=true, to_apply=%region_18.19 | all-reduce | flops 1 | bytes 8 | tf_op jit(solution)/shard_map/psum | solution.py:58
  491.2 3.8 fusion.66
  495.6 3.5 fusion.57
  (82 shorter events, 11.9 us)
Async XLA Ops:
  7.2 23.9 %all-gather.13.cloned.1.call-start = ((), (), s32[]{:S(2)}) async-start(), calls=%async_computation.12 | async-start | bytes 1638400 | tf_op jit(solution)/shard_map/all_gather | solution.py:40
  9.2 41.8 %all-gather.15.cloned.1.call-start = ((), (), s32[]{:S(2)}) async-start(), calls=%async_computation.13 | async-start | bytes 1638400 | tf_op jit(solution)/shard_map/all_gather | solution.py:40
  11.2 59.9 %all-gather.17.cloned.1.call-start = ((), (), s32[]{:S(2)}) async-start(), calls=%async_computation.14 | async-start | bytes 1638400 | tf_op jit(solution)/shard_map/all_gather | solution.py:40
  13.2 77.9 %all-gather.21.cloned.1.call-start = ((), (), s32[]{:S(2)}) async-start(), calls=%async_computation.16 | async-start | bytes 1638400 | tf_op jit(solution)/shard_map/all_gather | solution.py:40
  13.8 97.2 %all-gather.23.cloned.1.call-start = ((), (), s32[]{:S(2)}) async-start(), calls=%async_computation.17 | async-start | bytes 1638400 | tf_op jit(solution)/shard_map/all_gather | solution.py:40
  14.4 116.6 %all-gather.19.cloned.1.call-start = ((), (), s32[]{:S(2)}) async-start(), calls=%async_computation.15 | async-start | bytes 1638400 | tf_op jit(solution)/shard_map/all_gather | solution.py:40
  15.0 275.0 %reduce-scatter.9.cloned.1.call-start = ((), (), s32[]{:S(2)}) async-start(), calls=%async_computation.7 | async-start | bytes 1638400 | tf_op jit(solution)/shard_map/reduce_scatter | solution.py:43
  24.6 26.4 %copy-start.17 = (f32[4096]{0:T(1024)}, f32[4096]{0:T(1024)S(1)}, u32[]{:S(2)}) copy-start(f32[4096]{0:T(1024)S(1)} %add_rsqrt_fusion) | copy-start | bytes 49156
  131.0 28.9 %copy-start.2 = (bf16[4096,512]{0,1:T(8,128)(2,1)S(1)}, bf16[4096,512]{0,1:T(8,128)(2,1)}, u32[]{:S(2)}) copy-start(bf16[4096,512]{0,1:T(8,128)(2,1)} %get-tuple-element.33) | copy-start | bytes 12582916
  159.9 9.7 %copy-start.20 = (bf16[1,512,1280]{2,1,0:T(8,128)(2,1)S(1)}, bf16[1,512,1280]{2,1,0:T(8,128)(2,1)}, u32[]{:S(2)}) copy-start(bf16[1,512,1280]{2,1,0:T(8,128)(2,1)} %all-gather.23.cloned.1.call-done) | copy-start | bytes 3932164
  169.5 120.5 %reduce-scatter.7.cloned.1.call-start = ((), (), s32[]{:S(2)}) async-start(), calls=%async_computation.6 | async-start | bytes 1638400 | tf_op jit(solution)/shard_map/reduce_scatter | solution.py:43
  169.6 15.6 %copy-start.3 = (bf16[4096,512]{0,1:T(8,128)(2,1)S(1)}, bf16[4096,512]{0,1:T(8,128)(2,1)}, u32[]{:S(2)}) copy-start(bf16[4096,512]{0,1:T(8,128)(2,1)} %get-tuple-element.33) | copy-start | bytes 12582916
  169.6 15.5 %copy-start.21 = (bf16[1,512,1280]{2,1,0:T(8,128)(2,1)S(1)}, bf16[1,512,1280]{2,1,0:T(8,128)(2,1)}, u32[]{:S(2)}) copy-start(bf16[1,512,1280]{2,1,0:T(8,128)(2,1)} %all-gather.19.cloned.1.call-done) | copy-start | bytes 3932164
  185.1 11.2 %copy-start.1 = (bf16[1,4096,512]{1,2,0:T(8,128)(2,1)S(1)}, bf16[1,4096,512]{1,2,0:T(8,128)(2,1)}, u32[]{:S(2)}) copy-start(bf16[1,4096,512]{1,2,0:T(8,128)(2,1)} %copy.21) | copy-start | bytes 12582916
  199.2 8.4 %copy-start.4 = (bf16[4096,512]{0,1:T(8,128)(2,1)}, bf16[4096,512]{0,1:T(8,128)(2,1)S(1)}, u32[]{:S(2)}) copy-start(bf16[4096,512]{0,1:T(8,128)(2,1)S(1)} %fusion.25) | copy-start | bytes 12582916
  199.2 8.4 %copy-start = (bf16[1,4096,512]{1,2,0:T(8,128)(2,1)S(1)}, bf16[1,4096,512]{1,2,0:T(8,128)(2,1)}, u32[]{:S(2)}) copy-start(bf16[1,4096,512]{1,2,0:T(8,128)(2,1)} %copy.20) | copy-start | bytes 12582916
  199.2 8.4 %copy-start.18 = (f32[4096]{0:T(1024)S(1)}, f32[4096]{0:T(1024)}, u32[]{:S(2)}) copy-start(f32[4096]{0:T(1024)} %copy-done.17) | copy-start | bytes 49156
  228.2 61.8 %reduce-scatter.13.cloned.1.call-start = ((), (), s32[]{:S(2)}) async-start(), calls=%async_computation.9 | async-start | bytes 1638400 | tf_op jit(solution)/shard_map/reduce_scatter | solution.py:43
  244.6 68.8 %reduce-scatter.11.cloned.1.call-start = ((), (), s32[]{:S(2)}) async-start(), calls=%async_computation.8 | async-start | bytes 1638400 | tf_op jit(solution)/shard_map/reduce_scatter | solution.py:43
  260.9 81.9 %reduce-scatter.17.cloned.1.call-start = ((), (), s32[]{:S(2)}) async-start(), calls=%async_computation.11 | async-start | bytes 1638400 | tf_op jit(solution)/shard_map/reduce_scatter | solution.py:43
  279.4 92.8 %reduce-scatter.15.cloned.1.call-start = ((), (), s32[]{:S(2)}) async-start(), calls=%async_computation.10 | async-start | bytes 1638400 | tf_op jit(solution)/shard_map/reduce_scatter | solution.py:43
  289.9 201.2 %copy-start.5 = (bf16[2,320,512]{2,1,0:T(8,128)(2,1)S(1)}, bf16[2,320,512]{2,1,0:T(8,128)(2,1)}, u32[]{:S(2)}) copy-start(bf16[2,320,512]{2,1,0:T(8,128)(2,1)} %param.15) | copy-start | bytes 1966084
  289.9 201.2 %copy-start.8 = (f32[2,320,512]{2,1,0:T(8,128)S(1)}, f32[2,320,512]{2,1,0:T(8,128)}, u32[]{:S(2)}) copy-start(f32[2,320,512]{2,1,0:T(8,128)} %param.21) | copy-start | bytes 3932164
  289.9 185.5 %all-reduce.3.cloned.1.call-start = ((), (), s32[]{:S(2)}) async-start(), calls=%async_computation.18 | async-start | bytes 3932160 | tf_op jit(solution)/shard_map/psum | solution.py:43
  477.4 17.6 %copy-start.6 = (bf16[2,128,1280]{2,1,0:T(8,128)(2,1)S(1)}, bf16[2,128,1280]{2,1,0:T(8,128)(2,1)}, u32[]{:S(2)}) copy-start(bf16[2,128,1280]{2,1,0:T(8,128)(2,1)} %param.13) | copy-start | bytes 1966084
  477.4 17.6 %copy-start.7 = (bf16[2,128,1280]{2,1,0:T(8,128)(2,1)S(1)}, bf16[2,128,1280]{2,1,0:T(8,128)(2,1)}, u32[]{:S(2)}) copy-start(bf16[2,128,1280]{2,1,0:T(8,128)(2,1)} %param.14) | copy-start | bytes 1966084
  491.1 3.9 copy-start.9
  491.1 3.9 copy-start.10
  491.1 3.9 copy-start.11
  491.1 3.9 copy-start.12
  491.2 4.1 copy-start.15
  491.2 4.4 copy-start.16
  (3 other events, 10.6 us)
Sparse Core Ops, SparseCore 0:
  10.1 20.6 all-gather.12
  33.0 17.9 all-gather.14
  53.1 17.9 all-gather.16
  73.1 17.9 all-gather.20
  93.1 17.9 all-gather.22
  113.1 17.9 all-gather.18
  169.7 26.3 reduce-scatter.8
  228.3 26.3 reduce-scatter.6
  257.8 26.2 reduce-scatter.12
  287.1 26.2 reduce-scatter.10
  316.5 26.2 reduce-scatter.16
  345.8 26.2 reduce-scatter.14
  376.4 98.9 all-reduce.2
where the time goes:
time: 515 us; the launch traced here: 506 us
  waiting for transfers between devices  222 us (43%)
  matrix products  220 us (43%)
  local copies, waits for them, and re-layouts  19.4 us (4%)
  other arithmetic  19.3 us (4%)
  between operations  17.3 us (3%)
  blocking collectives  6.89 us (1%)
    psum x1, waiting for transfers between devices, summed(): lax.psum(lax.psum_scatter(term, 's', scatter_dimension=0, tiled=True), 'r')  103 us
    reduce_scatter x6, waiting for transfers between devices, summed(): lax.psum_scatter(term, 's', scatter_dimension=0, tiled=True)  82.1 us
    dot_general x5, matrix products, layer(): gate = jnp.dot(a, w['w_gate'], preferred_element_type=jnp.float32)  82.1 us
    dot_general x5, matrix products, layer(): up = jnp.dot(a, w['w_up'], preferred_element_type=jnp.float32)  79.1 us
    dot_general x5, matrix products, matmul(): jnp.dot(a, w, preferred_element_type=jnp.float32).astype(jnp.bfloat16)  59.1 us
    all_gather x6, waiting for transfers between devices, fetched(): lax.all_gather(w[number], 's', axis=0, tiled=True)  35.1 us
    unnamed x46, local copies, waits for them, and re-layouts  13.6 us
  transfers between devices with their start and end apart: 13, of which 9 were waited for; matrix products, arithmetic and copies ran while one was open for 40% of the time, Pallas kernels for 0%

commit v1 on v0

v1 whole, which is shorter than its diff:
```python
import functools

import jax
import jax.numpy as jnp
from jax import lax
from jax.experimental import pallas as pl
from jax.experimental.pallas import tpu as pltpu
from jax.sharding import PartitionSpec as P

MESH = pl.DeviceIdType.MESH
BF, F32 = jnp.bfloat16, jnp.float32
T, D, FF, L = 4096, 512, 1280, 2
TB, FC = 512, 256
NT, NC = T // TB, FF // FC
TBB = 1024
BB = T // TBB
G = L * NC
DS, FS = D // 4, FF // 4


def dot(a, b):
    return jnp.dot(a, b, preferred_element_type=F32)


def dot_t(a, b):
    return lax.dot_general(a, b, (((1,), (1,)), ((), ())), preferred_element_type=F32)


def sigmoid(g):
    return 0.5 + 0.5 * jnp.tanh(0.5 * g)


def norm_scale(wide):
    return lax.rsqrt(jnp.mean(wide * wide, -1, keepdims=True) + 1e-6)


def aligned(i, n):
    return pl.multiple_of(i * n, n)


def kernel(x_in, dy_in, wg_in, wu_in, wd_in, gu_out, d_out, sq_out, *scratch):
    (hb, dyb, a0, a1, a0t, a1t, dyt, da, wgu, wd, acc, sbg, sbd, r0g, r0d, t1g, t1d, r1g, r1d, o32g, o32d, s2g, s2d, r2g, r2d,
     fg, fd, gfin, dfin, sq, ld, wla, wcs, wcr, wxs, wxr, wys, wyr, was, war, wbs, wbr,
     s0s, s0r, s1s, s1r, s2s, s2r, s3s, s3r, s3ds, s3dr, sqs, sqr, osem) = scratch
    s, r = lax.axis_index("s"), lax.axis_index("r")
    xx, cc, yy = s // 2, s % 2, r // 4
    s1, s2, s3 = 2 * xx + 1 - cc, 2 * (1 - xx) + cc, 2 * (1 - xx) + 1 - cc
    across = (r + 4) % 8

    def remote(src, dst, send, recv, rr, ss):
        return pltpu.make_async_remote_copy(
            src_ref=src, dst_ref=dst, send_sem=send, recv_sem=recv, device_id={"r": rr, "s": ss}, device_id_type=MESH
        )

    barrier = pltpu.get_barrier_semaphore()
    for dr in (0, 4, 1, 7, 5, 3, 2, 6):
        for ds in range(4):
            if (dr, ds) != (0, 0):
                pl.semaphore_signal(barrier, inc=1, device_id={"r": (r + dr) % 8, "s": (s + ds) % 4}, device_id_type=MESH)

    WIDE = (512, 768)

    def first(part, x):
        return pl.multiple_of((1 - x) * 512, 256) if part else pl.multiple_of(x * 768, 256)

    def shard_in(j):
        return (wg_in, wu_in, wd_in)[j % 3].at[j // 3]

    def region(j, who):
        if j % 3 < 2:
            return wgu.at[j // 3, j % 3, pl.ds(aligned(who, DS), DS), :]
        return wd.at[j // 3, pl.ds(aligned(who, FS), FS), :]

    def own(j):
        return pltpu.make_async_copy(shard_in(j), region(j, s), wla.at[j])

    def to_core(j):
        return remote(region(j, s), region(j, s), wcs.at[j], wcr.at[j], r, s1)

    def half_of(j, who, half, x):
        if j < 4:
            return wgu.at[0, j % 2, pl.ds(aligned(2 * who + half, 64), 64), pl.ds(first(j // 2, x), WIDE[j // 2])]
        if j in (5, 6):
            return wgu.at[1, j - 5, pl.ds(aligned(2 * who + half, 64), 64), :]
        return wd.at[(j - 4) // 3, pl.ds(aligned(2 * who + half, 160), 160), :]

    def by_x(j):
        return remote(half_of(j, s, yy, 1 - xx), half_of(j, s, yy, 1 - xx), wxs.at[j], wxr.at[j], r, s2)

    def by_y(j):
        return remote(half_of(j, s2, yy, xx), half_of(j, s2, yy, xx), wys.at[j], wyr.at[j], across, s)

    def by_core(j, half, send, recv):
        return remote(half_of(j, s2, half, xx), half_of(j, s2, half, xx), send.at[j], recv.at[j], r, s1)

    def got_x(j):
        by_x(j).wait_recv()
        by_y(j).start()
        by_core(j, yy, was, war).start()

    def got_y(j):
        by_y(j).wait_recv()
        by_core(j, 1 - yy, wbs, wbr).start()

    def got_core(j):
        by_core(j, yy, was, war).wait_recv()
        by_core(j, 1 - yy, wbs, wbr).wait_recv()

    for j in range(6):
        own(j).start()
    load_x = pltpu.make_async_copy(x_in.at[0], hb, ld.at[0])
    load_dy = pltpu.make_async_copy(dy_in.at[0], dyb, ld.at[1])
    load_x.start()
    load_dy.start()
    for j in range(6):
        own(j).wait()
    pl.semaphore_wait(barrier, 31)
    for j in range(8):
        by_x(j).start()
    for j in range(6):
        to_core(j).start()
    load_x.wait()
    load_dy.wait()

    def prologue(i, _):
        rows = pl.ds(aligned(i, TB), TB)
        wide = hb[rows, :].astype(F32)
        a = (wide * norm_scale(wide)).astype(BF)
        a0[rows, :] = a
        a0t[:, rows] = a.T
        dyt[:, rows] = dyb[rows, :].T

        @pl.when(i == 4)
        def _():
            got_x(0)
            got_x(1)

        return 0

    lax.fori_loop(0, NT, prologue, 0)

    def mlp(a, start, width):
        o = None
        for c in range(width // FC):
            cols = pl.ds(pl.multiple_of(start + c * FC, FC), FC)
            g = dot(a, wgu[0, 0, :, cols])
            u = dot(a, wgu[0, 1, :, cols])
            p = (g * sigmoid(g) * u).astype(BF)
            one = dot(p, wd[0, cols, :])
            o = one if o is None else o + one
        return o

    def fwd_first(i, _):
        @pl.when(i == 2)
        def _():
            got_x(3)
            got_y(2)

        @pl.when(i == 5)
        def _():
            got_x(4)
            got_y(3)

        rows = pl.ds(aligned(i, TB), TB)
        da[rows, :] = mlp(a0[rows, :], first(0, xx), WIDE[0])
        return 0

    def fwd_second(i, _):
        @pl.when(i == 4)
        def _():
            for j in (5, 6, 7):
                got_x(j)

        @pl.when(i == 7)
        def _():
            for j in (5, 6, 7):
                got_y(j)

        rows = pl.ds(aligned(i, TB), TB)
        o = da[rows, :] + mlp(a0[rows, :], first(1, xx), WIDE[1])
        da[rows, :] = jnp.zeros((TB, D), F32)
        h = hb[rows, :] + o.astype(BF)
        hb[rows, :] = h
        wide = h.astype(F32)
        a = (wide * norm_scale(wide)).astype(BF)
        a1[rows, :] = a
        a1t[:, rows] = a.T
        return 0

    got_y(0)
    got_y(1)
    got_x(2)
    for j in range(3):
        to_core(j).wait_recv()
    got_core(0)
    got_core(1)
    lax.fori_loop(0, NT, fwd_first, 0)
    got_y(4)
    for j in (2, 3, 4):
        got_core(j)
    lax.fori_loop(0, NT, fwd_second, 0)
    for j in range(3, 6):
        to_core(j).wait_recv()
    for j in (5, 6, 7):
        got_core(j)

    def part(m, who):
        return pl.ds(aligned(who, 64), 64) if m == 2 else pl.ds(aligned(who, DS), DS)

    def mine(m, gu, d):
        return (lambda g, *at: d.at[(g, *at)]) if m == 2 else (lambda g, *at: gu.at[(g, m, *at)])

    def stage0(g, m, w):
        slot = g % 2
        src = mine(m, sbg, sbd)(slot, part(m, (s1, s3)[w]), slice(None))
        return remote(src, mine(m, r0g, r0d)(slot, w), s0s.at[slot, m // 2], s0r.at[slot, 2 * m + w], r, s1)

    def stage0_sent(g):
        slot = g % 2
        pltpu.make_async_copy(r0g.at[slot], r0g.at[slot], s0s.at[slot, 0]).wait()
        pltpu.make_async_copy(r0d.at[slot], r0d.at[slot], s0s.at[slot, 1]).wait()

    def stage1(g, m):
        return remote(mine(m, t1g, t1d)(g % 2), mine(m, r1g, r1d)(g), s1s.at[g % 2, m], s1r.at[g, m], r, s2)

    def piece(m, who):
        if m == 2:
            return pl.ds(aligned(who // 2, 16), 16), pl.ds(aligned(who % 2, 256), 256)
        return pl.ds(aligned(who, 16), 16), slice(None)

    def stage2(g, m, k):
        to = (r + k) % 8
        return remote(
            mine(m, s2g, s2d)(g, *piece(m, to)), mine(m, r2g, r2d)(g, k - 1), s2s.at[m // 2], s2r.at[g, 7 * m + k - 1], to, s
        )

    def place(g):
        block = 4 * (g % NC) + s
        spot = pl.ds(aligned(4 * (block % 5) + r // 2, 16), 16), pl.ds(aligned(r % 2, 256), 256)
        return 1 - g // NC, g % NC, block // 5, spot

    def stage3(g, m, k):
        to = (r + k) % 8
        layer, c, owner, spot = place(g)
        if m == 2:
            return remote(fd.at[g], dfin.at[(layer, *spot)], s3ds, s3dr, to, owner)
        return remote(fg.at[g, m], gfin.at[layer, m, pl.ds(aligned(r, 16), 16), pl.ds(aligned(c, FC), FC)], s3s, s3r, to, s)

    def add0(g, m, fresh):
        slot = g % 2
        for w in (1, 0):
            stage0(g, m, w).wait_recv()
        if not fresh:
            stage1(g, m).wait_send()
        own_term = mine(m, sbg, sbd)
        arrived = mine(m, r0g, r0d)
        other = own_term(slot, part(m, s2), slice(None))[...].astype(F32) + arrived(slot, 1)[...].astype(F32)
        mine(m, t1g, t1d)(slot)[...] = other.astype(BF)
        stage1(g, m).start()
        kept = own_term(slot, part(m, s), slice(None))[...].astype(F32) + arrived(slot, 0)[...].astype(F32)
        mine(m, o32g, o32d)(g % 4)[...] = kept

    def add1(g, m):
        stage1(g, m).wait_recv()
        total = mine(m, o32g, o32d)(g % 4)[...] + mine(m, r1g, r1d)(g)[...].astype(F32)
        mine(m, o32g, o32d)(g % 4)[...] = total
        mine(m, s2g, s2d)(g)[...] = total.astype(BF)
        for k in (4, 5, 3, 6, 2, 7, 1):
            stage2(g, m, k).start()

    def add2(g, m):
        for k in range(1, 8):
            stage2(g, m, k).wait_recv()
        total = mine(m, o32g, o32d)(g % 4, *piece(m, r))[...]
        for k in range(7):
            total += mine(m, r2g, r2d)(g, k)[...].astype(F32)
        total = total.astype(BF)
        mine(m, fg, fd)(g)[...] = total
        layer, c, owner, spot = place(g)
        if m == 2:

            @pl.when(owner == s)
            def _():
                dfin[(layer, *spot)] = total

            @pl.when(owner != s)
            def _():
                stage3(g, m, 0).start()
        else:
            gfin[layer, m, pl.ds(aligned(r, 16), 16), pl.ds(aligned(c, FC), FC)] = total
        for k in (4, 5, 3, 6, 2, 7, 1):
            stage3(g, m, k).start()

    def backward(layer, a_ref, at_ref, with_da):
        def chunk(c, _):
            cols = pl.ds(aligned(c, FC), FC)
            n = (1 - layer) * NC + c

            def block(i, _):
                @pl.when((i == 1) & (n >= 3))
                def _():
                    for m in range(3):
                        add0(n - 1, m, False)

                @pl.when((i == 1) & (n >= 1) & (n < 3))
                def _():
                    for m in range(3):
                        add0(n - 1, m, True)

                @pl.when((i == BB - 1) & (n >= 2))
                def _():
                    for m in range(3):
                        add2(n - 2, m)

                @pl.when((i == BB - 1) & (n >= 1))
                def _():
                    for m in range(3):
                        add1(n - 1, m)

                rows = pl.ds(aligned(i, TBB), TBB)
                a = a_ref[rows, :]
                g = dot(a, wgu[layer, 0, :, cols])
                u = dot(a, wgu[layer, 1, :, cols])
                dp = dot_t(dyb[rows, :], wd[layer, cols, :]).astype(BF).astype(F32)
                sig = sigmoid(g)
                sl = g * sig
                p = (sl * u).astype(BF)
                du = (dp * sl).astype(BF)
                dg = (dp * u * (sig + sl * (1.0 - sig))).astype(BF)
                for m, (left, right) in enumerate(((at_ref, dg), (at_ref, du), (dyt, p))):
                    acc[m] = jnp.where(i > 0, acc[m], 0.0) + dot(left[:, rows], right)
                if with_da:
                    da[rows, :] += dot_t(dg, wgu[layer, 0, :, cols]) + dot_t(du, wgu[layer, 1, :, cols])
                return 0

            lax.fori_loop(0, BB, block, 0)
            slot = n % 2

            @pl.when(n >= 2)
            def _():
                stage0_sent(n)

            for m in range(3):
                mine(m, sbg, sbd)(slot)[...] = (acc[m].T if m == 2 else acc[m]).astype(BF)
                for w in (1, 0):
                    stage0(n, m, w).start()
            return 0

        lax.fori_loop(0, NC, chunk, 0)

    backward(1, a1, a1t, True)

    def norm_back(i, _):
        rows = pl.ds(aligned(i, TB), TB)
        wide = hb[rows, :].astype(F32)
        scale = norm_scale(wide)
        t = da[rows, :].astype(BF).astype(F32)
        back = scale * t - wide * (scale * scale * scale * jnp.mean(t * wide, -1, keepdims=True))
        dh = dyb[rows, :] + back.astype(BF)
        dyb[rows, :] = dh
        dyt[:, rows] = dh.T
        return 0

    lax.fori_loop(0, NT, norm_back, 0)
    backward(0, a0, a0t, False)

    for m in range(3):
        add0(G - 1, m, False)
    for m in range(3):
        add2(G - 2, m)
    for m in range(3):
        add1(G - 1, m)
    for m in range(3):
        add2(G - 1, m)

    def bytes_of(ref, sem):
        pltpu.make_async_copy(ref, ref, sem).wait()

    bytes_of(gfin.at[:, :, 0 : 7 * 16, :], s3r)
    bytes_of(dfin.at[:, 0:304, :], s3dr)
    out_g = pltpu.make_async_copy(gfin, gu_out, osem.at[0])
    out_d = pltpu.make_async_copy(dfin, d_out, osem.at[1])
    out_g.start()
    out_d.start()

    def squares(n, width, read):
        def one(i, total):
            v = read(i).astype(F32)
            return total + jnp.sum((v * v).reshape(n // 8, 8, width), axis=0)

        return one

    tg = jnp.zeros((8, FF), F32)
    td = jnp.zeros((8, D), F32)
    for layer in range(L):
        for m in range(2):
            tg = lax.fori_loop(0, DS // 32, squares(32, FF, lambda i: gfin[layer, m, pl.ds(aligned(i, 32), 32), :]), tg)
        td = lax.fori_loop(0, FS // 64, squares(64, D, lambda i: dfin[layer, pl.ds(aligned(i, 64), 64), :]), td)
    total = jnp.zeros((8, 128), F32)
    for j in range(FF // 128):
        total += tg[:, 128 * j : 128 * j + 128]
    for j in range(D // 128):
        total += td[:, 128 * j : 128 * j + 128]
    sq[s] = total

    def share(k, whose):
        return remote(sq.at[s], sq.at[whose], sqs.at[k - 1], sqr.at[k - 1], r, (s + k) % 4)

    for k in (2, 3, 1):
        share(k, s).start()
    for j in range(6):
        to_core(j).wait_send()
    for j in range(8):
        by_x(j).wait_send()
        by_y(j).wait_send()
        by_core(j, yy, was, war).wait_send()
        by_core(j, 1 - yy, wbs, wbr).wait_send()
    stage0_sent(G - 2)
    stage0_sent(G - 1)
    for m in range(3):
        stage1(G - 2, m).wait_send()
        stage1(G - 1, m).wait_send()
    bytes_of(r2g, s2s.at[0])
    bytes_of(r2d, s2s.at[1])
    bytes_of(gfin.at[:, :, 0 : 7 * 16, :], s3s)
    bytes_of(dfin.at[:, 0:304, :], s3ds)
    for k in (1, 2, 3):
        share(k, (s + 4 - k) % 4).wait()
    sq_out[...] = ((sq[0] + sq[1]) + sq[2]) + sq[3]
    out_g.wait()
    out_d.wait()


def adamw(w, m, v, g):
    m = 0.9 * m + 0.1 * g
    v = 0.95 * v + 0.05 * g * g
    step = m * lax.rsqrt(v + 1e-8) + 0.1 * w
    return (w - 0.02 * step).astype(BF), m, v


def solution(mesh):
    def step(x, dy, *arrays):
        weights, ms, vs = (arrays[i : i + 3] for i in (0, 3, 6))
        hbm = pl.BlockSpec(memory_space=pl.ANY)
        dma = pltpu.SemaphoreType.DMA
        gu, d, sq = pl.pallas_call(
            kernel,
            name="train_step",
            out_shape=(
                jax.ShapeDtypeStruct((L, 2, DS, FF), BF),
                jax.ShapeDtypeStruct((L, FS, D), BF),
                jax.ShapeDtypeStruct((8, 128), F32),
            ),
            in_specs=[hbm] * 5,
            out_specs=(hbm, hbm, pl.BlockSpec(memory_space=pltpu.VMEM)),
            scratch_shapes=[
                pltpu.VMEM((T, D), BF),
                pltpu.VMEM((T, D), BF),
                pltpu.VMEM((T, D), BF),
                pltpu.VMEM((T, D), BF),
                pltpu.VMEM((D, T), BF),
                pltpu.VMEM((D, T), BF),
                pltpu.VMEM((D, T), BF),
                pltpu.VMEM((T, D), F32),
                pltpu.VMEM((L, 2, D, FF), BF),
                pltpu.VMEM((L, FF, D), BF),
                pltpu.VMEM((3, D, FC), F32),
                pltpu.VMEM((2, 2, D, FC), BF),
                pltpu.VMEM((2, FC, D), BF),
                pltpu.VMEM((2, 2, 2, DS, FC), BF),
                pltpu.VMEM((2, 2, FC // 4, D), BF),
                pltpu.VMEM((2, 2, DS, FC), BF),
                pltpu.VMEM((2, FC // 4, D), BF),
                pltpu.VMEM((G, 2, DS, FC), BF),
                pltpu.VMEM((G, FC // 4, D), BF),
                pltpu.VMEM((4, 2, DS, FC), F32),
                pltpu.VMEM((4, FC // 4, D), F32),
                pltpu.VMEM((G, 2, DS, FC), BF),
                pltpu.VMEM((G, FC // 4, D), BF),
                pltpu.VMEM((G, 2, 7, 16, FC), BF),
                pltpu.VMEM((G, 7, 16, 256), BF),
                pltpu.VMEM((G, 2, 16, FC), BF),
                pltpu.VMEM((G, 16, 256), BF),
                pltpu.VMEM((L, 2, DS, FF), BF),
                pltpu.VMEM((L, FS, D), BF),
                pltpu.VMEM((4, 8, 128), F32),
                dma((2,)),
                dma((6,)), dma((6,)), dma((6,)),
                dma((8,)), dma((8,)), dma((8,)), dma((8,)), dma((8,)), dma((8,)), dma((8,)), dma((8,)),
                dma((2, 2)), dma((2, 6)), dma((2, 3)), dma((G, 3)),
                dma((2,)), dma((G, 21)),
                dma(()), dma(()), dma(()), dma(()),
                dma((3,)), dma((3,)), dma((2,)),
            ],
            compiler_params=pltpu.CompilerParams(collective_id=0, has_side_effects=True, vmem_limit_bytes=67043328),
        )(x, dy, *weights)
        count = 4 * (gu.size + d.size)
        factor = jnp.minimum(1.0, 0.5 * lax.rsqrt(jnp.sum(sq) / count + 1e-30))
        grads = (gu[:, 0], gu[:, 1], d)
        new = [adamw(w.astype(F32), m, v, g.astype(F32) * factor) for w, m, v, g in zip(weights, ms, vs, grads, strict=True)]
        return tuple(one[which] for which in range(3) for one in new)

    states, cut = P(("rep", "r", "s"), None, None), P(None, "s", None)
    return jax.shard_map(
        step, mesh=mesh, in_specs=(states, states) + (cut,) * 9, out_specs=(P("rep", "s", None),) * 9, check_vma=False
    )
```

time: 515 us -> 207 us (0.40); the launches traced: 506 us -> 207 us
  waiting for transfers between devices: 222 us -> 0 us
  matrix products: 220 us -> 0 us
  Pallas kernels: 0 us -> 195 us
  local copies, waits for them, and re-layouts: 19.4 us -> 0.02 us
  between operations: 17.3 us -> 1.4 us
  other arithmetic: 19.3 us -> 10.3 us
  blocking collectives: 6.89 us -> 0 us
    dot_general x15 -> x0, matrix products: 220 us -> none  [the longest x5 82.1 us: layer(): gate = jnp.dot(a, w['w_gate'], preferred_element_type=jnp.float32)]
    pallas_call x0 -> x1, Pallas kernels: none -> 195 us  [step(): pl.pallas_call(kernel, name='train_step', out_shape=(jax.ShapeDtypeStruct...]
    psum x1 -> x0, waiting for transfers between devices: 103 us -> none  [summed(): lax.psum(lax.psum_scatter(term, 's', scatter_dimension=0, tiled=True), 'r')]
    reduce_scatter x6 -> x0, waiting for transfers between devices: 82.1 us -> none  [summed(): lax.psum_scatter(term, 's', scatter_dimension=0, tiled=True)]
    all_gather x6 -> x0, waiting for transfers between devices: 35.1 us -> none  [fetched(): lax.all_gather(w[number], 's', axis=0, tiled=True)]
    unnamed x46 -> x8, local copies, waits for them, and re-layouts: 13.6 us -> 0.02 us
    reduce_sum x4 -> x1, other arithmetic: 9.21 us -> 1.28 us  [step(): factor = jnp.minimum(1.0, 0.5 * lax.rsqrt(jnp.sum(sq) / count + 1e-30))]
    psum x1 -> x0, blocking collectives: 6.89 us -> none  [step(): squares = lax.psum(sum((jnp.sum(g * g) for g in gradients)), 's')]
  transfers between devices with their start and end apart: 13 -> 0, of which waited for: 9 -> 0; matrix products, arithmetic and copies ran while one was open for 40% -> 0% of each run, Pallas kernels for 0% -> 0%
where the time goes in v1:
time: 207 us
  Pallas kernels  195 us (94%)
  other arithmetic  10.3 us (5%)
    pallas_call x1, Pallas kernels, step(): pl.pallas_call(kernel, name='train_step', out_shape=(jax.ShapeDtypeStruct...  195 us
    convert_element_type x2, other arithmetic, adamw(): return ((w - 0.02 * step).astype(BF), m, v)  8.99 us

profile of v1, /device:TPU:0, one launch (start us, length us, event | category | flops | bytes accessed | tf_op | source)
XLA Modules:
  0.0 206.7 jit_solution(11787576451783211073)
XLA Ops:
  0.6 195.0 %train_step.1 = (bf16[2,2,128,1280]{3,2,1,0:T(8,128)(2,1)}, bf16[2,320,512]{2,1,0:T(8,128)(2,1)}, f32[8,128]{1,0:T(8,128)}) custom-call(bf16[1,4096,512]{2,1,0:T(8,128)(2,1)} %x_in.1, bf16[1,4096,512]{2,1,0:T(8,128)(2,1)} %dy_in.1, bf16[2,128,1280]{2,1,0:T(8,128)(2,1)} %wg_in.1, bf16[2,128,1280]{2,1,0:T(8,128)(2,1)} %wu_in.1, bf16[2,320,512]{2,1,0:T(8,128)(2,1)} %wd_in.1), custom_call_target="tpu_custom_call" | custom-call | tf_op jit(solution)/shard_map/train_step/pallas_call | solution.py:446
  195.7 1.3 reduce_sum.9
  197.7 0.0 copy-start
  197.7 0.0 copy-start.1
  197.7 0.0 copy-start.2
  197.7 0.0 copy-start.3
  197.7 6.9 %fusion.2 = (bf16[2,128,1280]{2,1,0:T(8,128)(2,1)}, f32[2,128,1280]{2,1,0:T(8,128)}, f32[2,128,1280]{2,1,0:T(8,128)}, bf16[2,128,1280]{2,1,0:T(8,128)(2,1)}, f32...) fusion(bf16[2,128,1280]{2,1,0:T(8,128)(2,1)} %wg_in.1, f32[]{:T(128)S(6)} %min_shard_map.3, f32[2,128,1280]{2,1,0:T(8,128)} %param.19, ...), kind=kLoop, calls=%fused_computation.11 | loop fusion | flops 11141120 | bytes 14417924 | tf_op jit(solution)/shard_map/convert_element_type | solution.py:438
  204.6 0.0 copy-done
  204.6 0.0 copy-done.1
  204.6 0.0 copy-done.2
  204.6 0.0 copy-done.3
  204.6 2.1 %fusion.8 = (bf16[2,320,512]{2,1,0:T(8,128)(2,1)}, f32[2,320,512]{2,1,0:T(8,128)}, f32[2,320,512]{2,1,0:T(8,128)}) fusion(bf16[2,320,512]{2,1,0:T(8,128)(2,1)S(1)} %copy-done, f32[]{:T(128)S(6)} %min_shard_map.3, bf16[2,320,512]{2,1,0:T(8,128)(2,1)S(1)} %copy-done.3, f32[2,320,512]{2,1,0:T(8,128)S(1)} %copy-done.1, f32[2,320,512]{2,1,0:T(8,128)S(1)} %copy-done.2), kind=kLoop, calls=%fused_computation.17 | loop fusion | flops 5570560 | bytes 7208964 | tf_op jit(solution)/shard_map/convert_element_type | solution.py:438
Async XLA Ops:
  197.7 6.9 %copy-start = (bf16[2,320,512]{2,1,0:T(8,128)(2,1)S(1)}, bf16[2,320,512]{2,1,0:T(8,128)(2,1)}, u32[]{:S(2)}) copy-start(bf16[2,320,512]{2,1,0:T(8,128)(2,1)} %wd_in.1) | copy-start | bytes 1966084
  197.7 6.9 %copy-start.1 = (f32[2,320,512]{2,1,0:T(8,128)S(1)}, f32[2,320,512]{2,1,0:T(8,128)}, u32[]{:S(2)}) copy-start(f32[2,320,512]{2,1,0:T(8,128)} %param.21) | copy-start | bytes 3932164
  197.7 6.9 %copy-start.2 = (f32[2,320,512]{2,1,0:T(8,128)S(1)}, f32[2,320,512]{2,1,0:T(8,128)}, u32[]{:S(2)}) copy-start(f32[2,320,512]{2,1,0:T(8,128)} %param.18) | copy-start | bytes 3932164
  197.7 6.9 %copy-start.3 = (bf16[2,320,512]{2,1,0:T(8,128)(2,1)S(1)}, bf16[2,320,512]{2,1,0:T(8,128)(2,1)}, u32[]{:S(2)}) copy-start(bf16[2,320,512]{2,1,0:T(8,128)(2,1)} %get-tuple-element.14) | copy-start | bytes 1966084

commit v2 on v1

--- a/solution.py
+++ b/solution.py
@@ -12,9 +12,10 @@
 T, D, FF, L = 4096, 512, 1280, 2
 TB, FC = 512, 256
 NT, NC = T // TB, FF // FC
-TBB = 1024
+TBB, SB = 1024, 256
 BB = T // TBB
 G = L * NC
+STEPS = 4
 DS, FS = D // 4, FF // 4
 
 
@@ -39,9 +40,9 @@
 
 
 def kernel(x_in, dy_in, wg_in, wu_in, wd_in, gu_out, d_out, sq_out, *scratch):
-    (hb, dyb, a0, a1, a0t, a1t, dyt, da, wgu, wd, acc, sbg, sbd, r0g, r0d, t1g, t1d, r1g, r1d, o32g, o32d, s2g, s2d, r2g, r2d,
-     fg, fd, gfin, dfin, sq, ld, wla, wcs, wcr, wxs, wxr, wys, wyr, was, war, wbs, wbr,
-     s0s, s0r, s1s, s1r, s2s, s2r, s3s, s3r, s3ds, s3dr, sqs, sqr, osem) = scratch
+    (hb, dyb, a0, a1, a0t, a1t, dyt, da, wgu, wd, acc, sbg, sbd, r0g, r0d, t1g, t1d, r1g, r1d, o32g, o32d, s2g, s2d, ryg, ryd, r2g, r2d,
+     fg, fd, gfin, dfin, sqacc, sq, ld, wla, wcs, wcr, wxs, wxr, wys, wyr, was, war, wbs, wbr,
+     s0s, s0r, s1s, s1r, sys, syr, s2s, s2r, s3s, s3r, s3ds, s3dr, sqs, sqr, osem) = scratch
     s, r = lax.axis_index("s"), lax.axis_index("r")
     xx, cc, yy = s // 2, s % 2, r // 4
     s1, s2, s3 = 2 * xx + 1 - cc, 2 * (1 - xx) + cc, 2 * (1 - xx) + 1 - cc
@@ -78,11 +79,12 @@
         return remote(region(j, s), region(j, s), wcs.at[j], wcr.at[j], r, s1)
 
     def half_of(j, who, half, x):
-        if j < 4:
-            return wgu.at[0, j % 2, pl.ds(aligned(2 * who + half, 64), 64), pl.ds(first(j // 2, x), WIDE[j // 2])]
-        if j in (5, 6):
-            return wgu.at[1, j - 5, pl.ds(aligned(2 * who + half, 64), 64), :]
-        return wd.at[(j - 4) // 3, pl.ds(aligned(2 * who + half, 160), 160), :]
+        if j in (2, 7):
+            return wd.at[j // 7, pl.ds(aligned(2 * who + half, 160), 160), :]
+        rows = pl.ds(aligned(2 * who + half, 64), 64)
+        if j < 5:
+            return wgu.at[0, j % 3 if j < 2 else j - 3, rows, pl.ds(first(j // 3, x), WIDE[j // 3])]
+        return wgu.at[1, (j - 5) % 3, rows, slice(0, FC) if j < 7 else slice(FC, FF)]
 
     def by_x(j):
         return remote(half_of(j, s, yy, 1 - xx), half_of(j, s, yy, 1 - xx), wxs.at[j], wxr.at[j], r, s2)
@@ -106,6 +108,7 @@
         by_core(j, yy, was, war).wait_recv()
         by_core(j, 1 - yy, wbs, wbr).wait_recv()
 
+    sqacc[...] = jnp.zeros_like(sqacc)
     for j in range(6):
         own(j).start()
     load_x = pltpu.make_async_copy(x_in.at[0], hb, ld.at[0])
@@ -115,7 +118,7 @@
     for j in range(6):
         own(j).wait()
     pl.semaphore_wait(barrier, 31)
-    for j in range(8):
+    for j in range(10):
         by_x(j).start()
     for j in range(6):
         to_core(j).start()
@@ -130,10 +133,9 @@
         a0t[:, rows] = a.T
         dyt[:, rows] = dyb[rows, :].T
 
-        @pl.when(i == 4)
+        @pl.when(i == 6)
         def _():
             got_x(0)
-            got_x(1)
 
         return 0
 
@@ -154,27 +156,38 @@
         @pl.when(i == 2)
         def _():
             got_x(3)
-            got_y(2)
 
         @pl.when(i == 5)
         def _():
             got_x(4)
-            got_y(3)
 
         rows = pl.ds(aligned(i, TB), TB)
         da[rows, :] = mlp(a0[rows, :], first(0, xx), WIDE[0])
         return 0
 
     def fwd_second(i, _):
-        @pl.when(i == 4)
-        def _():
-            for j in (5, 6, 7):
-                got_x(j)
-
-        @pl.when(i == 7)
-        def _():
-            for j in (5, 6, 7):
-                got_y(j)
+        @pl.when(i == 0)
+        def _():
+            got_x(5)
+            got_x(6)
+
+        @pl.when(i == 1)
+        def _():
+            got_x(7)
+
+        @pl.when(i == 2)
+        def _():
+            got_y(5)
+            got_y(6)
+
+        @pl.when(i == 3)
+        def _():
+            got_x(8)
+
+        @pl.when(i == 5)
+        def _():
+            got_x(9)
+            got_y(7)
 
         rows = pl.ds(aligned(i, TB), TB)
         o = da[rows, :] + mlp(a0[rows, :], first(1, xx), WIDE[1])
@@ -187,6 +200,7 @@
         a1t[:, rows] = a.T
         return 0
 
+    got_x(1)
     got_y(0)
     got_y(1)
     got_x(2)
@@ -195,7 +209,8 @@
     got_core(0)
     got_core(1)
     lax.fori_loop(0, NT, fwd_first, 0)
-    got_y(4)
+    for j in (2, 3, 4):
+        got_y(j)
     for j in (2, 3, 4):
         got_core(j)
     lax.fori_loop(0, NT, fwd_second, 0)
@@ -228,10 +243,18 @@
             return pl.ds(aligned(who // 2, 16), 16), pl.ds(aligned(who % 2, 256), 256)
         return pl.ds(aligned(who, 16), 16), slice(None)
 
+    def half(m, y):
+        return pl.ds(aligned(y, 32), 32) if m == 2 else pl.ds(aligned(y, 64), 64)
+
+    def stage2y(g, m):
+        return remote(
+            mine(m, s2g, s2d)(g, half(m, 1 - yy), slice(None)), mine(m, ryg, ryd)(g), sys.at[m // 2], syr.at[g, m], across, s
+        )
+
     def stage2(g, m, k):
-        to = (r + k) % 8
+        to = 4 * yy + (r % 4 + k) % 4
         return remote(
-            mine(m, s2g, s2d)(g, *piece(m, to)), mine(m, r2g, r2d)(g, k - 1), s2s.at[m // 2], s2r.at[g, 7 * m + k - 1], to, s
+            mine(m, s2g, s2d)(g, *piece(m, to)), mine(m, r2g, r2d)(g, k - 1), s2s.at[m // 2], s2r.at[g, 3 * m + k - 1], to, s
         )
 
     def place(g):
@@ -265,17 +288,28 @@
         total = mine(m, o32g, o32d)(g % 4)[...] + mine(m, r1g, r1d)(g)[...].astype(F32)
         mine(m, o32g, o32d)(g % 4)[...] = total
         mine(m, s2g, s2d)(g)[...] = total.astype(BF)
-        for k in (4, 5, 3, 6, 2, 7, 1):
+        stage2y(g, m).start()
+
+    def add2y(g, m):
+        stage2y(g, m).wait_recv()
+        here = half(m, yy), slice(None)
+        total = mine(m, o32g, o32d)(g % 4, *here)[...] + mine(m, ryg, ryd)(g)[...].astype(F32)
+        mine(m, o32g, o32d)(g % 4, *here)[...] = total
+        mine(m, s2g, s2d)(g, *here)[...] = total.astype(BF)
+        for k in (2, 3, 1):
             stage2(g, m, k).start()
 
     def add2(g, m):
-        for k in range(1, 8):
+        for k in range(1, 4):
             stage2(g, m, k).wait_recv()
         total = mine(m, o32g, o32d)(g % 4, *piece(m, r))[...]
-        for k in range(7):
+        for k in range(3):
             total += mine(m, r2g, r2d)(g, k)[...].astype(F32)
         total = total.astype(BF)
         mine(m, fg, fd)(g)[...] = total
+        square = total.astype(F32)
+        square = square * square
+        sqacc[...] += (square[:8, :128] + square[:8, 128:]) + (square[8:, :128] + square[8:, 128:])
         layer, c, owner, spot = place(g)
         if m == 2:
 
@@ -297,40 +331,65 @@
             n = (1 - layer) * NC + c
 
             def block(i, _):
+                @pl.when((i == 0) & (n >= 2))
+                def _():
+                    for m in range(3):
+                        add1(n - 2, m)
+
                 @pl.when((i == 1) & (n >= 3))
                 def _():
                     for m in range(3):
                         add0(n - 1, m, False)
+                        add2(n - 3, m)
 
                 @pl.when((i == 1) & (n >= 1) & (n < 3))
                 def _():
                     for m in range(3):
                         add0(n - 1, m, True)
 
-                @pl.when((i == BB - 1) & (n >= 2))
+                @pl.when((i == 2) & (n >= 2))
                 def _():
                     for m in range(3):
-                        add2(n - 2, m)
-
-                @pl.when((i == BB - 1) & (n >= 1))
-                def _():
-                    for m in range(3):
-                        add1(n - 1, m)
-
-                rows = pl.ds(aligned(i, TBB), TBB)
-                a = a_ref[rows, :]
-                g = dot(a, wgu[layer, 0, :, cols])
-                u = dot(a, wgu[layer, 1, :, cols])
-                dp = dot_t(dyb[rows, :], wd[layer, cols, :]).astype(BF).astype(F32)
-                sig = sigmoid(g)
-                sl = g * sig
-                p = (sl * u).astype(BF)
-                du = (dp * sl).astype(BF)
-                dg = (dp * u * (sig + sl * (1.0 - sig))).astype(BF)
-                for m, (left, right) in enumerate(((at_ref, dg), (at_ref, du), (dyt, p))):
-                    acc[m] = jnp.where(i > 0, acc[m], 0.0) + dot(left[:, rows], right)
+                        add2y(n - 2, m)
+
                 if with_da:
-                    da[rows, :] += dot_t(dg, wgu[layer, 0, :, cols]) + dot_t(du, wgu[layer, 1, :, cols])
+
+                    @pl.when((i == 1) & (n == 0))
+                    def _():
+                        got_y(8)
+
+                    @pl.when((i == 2) & (n == 0))
+                    def _():
+                        got_y(9)
+
+                    @pl.when((i == 3) & (n == 0))
+                    def _():
+                        got_core(8)
+                        got_core(9)
+
+                def rows(q):
+                    return pl.ds(aligned(i * (TBB // SB) + q, SB), SB)
+
+                def front(q):
+                    a = a_ref[rows(q), :]
+                    g = dot(a, wgu[layer, 0, :, cols])
+                    u = dot(a, wgu[layer, 1, :, cols])
+                    dp = dot_t(dyb[rows(q), :], wd[layer, cols, :]).astype(BF).astype(F32)
+                    sig = sigmoid(g)
+                    sl = g * sig
+                    dsl = sig + sl * (1.0 - sig)
+                    return (dp * u * dsl).astype(BF), (dp * sl).astype(BF), (sl * u).astype(BF)
+
+                def back(qs, of):
+                    for m, left in enumerate((at_ref, at_ref, dyt)):
+                        base = jnp.where(i > 0, acc[m], 0.0) if qs[0] == 0 else acc[m]
+                        acc[m] = base + sum(dot(left[:, rows(q)], of[q][m]) for q in qs)
+                    if with_da:
+                        for q in qs:
+                            da[rows(q), :] += dot_t(of[q][0], wgu[layer, 0, :, cols]) + dot_t(of[q][1], wgu[layer, 1, :, cols])
+
+                of = [front(q) for q in range(4)]
+                back((0, 1, 2, 3), of)
                 return 0
 
             lax.fori_loop(0, BB, block, 0)
@@ -364,14 +423,17 @@
     lax.fori_loop(0, NT, norm_back, 0)
     backward(0, a0, a0t, False)
 
-    for m in range(3):
-        add0(G - 1, m, False)
-    for m in range(3):
-        add2(G - 2, m)
-    for m in range(3):
-        add1(G - 1, m)
-    for m in range(3):
-        add2(G - 1, m)
+    for which, g in ((add1, G - 2), (add2, G - 3), (functools.partial(add0, fresh=False), G - 1), (add2y, G - 2), (add1, G - 1),
+                     (add2, G - 2), (add2y, G - 1), (add2, G - 1)):
+        for m in range(3):
+            which(g, m)
+
+    me = 4 * r + s
+    sq[me] = sqacc[...]
+    for dr in range(8):
+        for ds in range(4):
+            if (dr, ds) != (0, 0):
+                remote(sq.at[me], sq.at[me], sqs, sqr, (r + dr) % 8, (s + ds) % 4).start()
 
     def bytes_of(ref, sem):
         pltpu.make_async_copy(ref, ref, sem).wait()
@@ -383,34 +445,14 @@
     out_g.start()
     out_d.start()
 
-    def squares(n, width, read):
-        def one(i, total):
-            v = read(i).astype(F32)
-            return total + jnp.sum((v * v).reshape(n // 8, 8, width), axis=0)
-
-        return one
-
-    tg = jnp.zeros((8, FF), F32)
-    td = jnp.zeros((8, D), F32)
-    for layer in range(L):
-        for m in range(2):
-            tg = lax.fori_loop(0, DS // 32, squares(32, FF, lambda i: gfin[layer, m, pl.ds(aligned(i, 32), 32), :]), tg)
-        td = lax.fori_loop(0, FS // 64, squares(64, D, lambda i: dfin[layer, pl.ds(aligned(i, 64), 64), :]), td)
-    total = jnp.zeros((8, 128), F32)
-    for j in range(FF // 128):
-        total += tg[:, 128 * j : 128 * j + 128]
-    for j in range(D // 128):
-        total += td[:, 128 * j : 128 * j + 128]
-    sq[s] = total
-
-    def share(k, whose):
-        return remote(sq.at[s], sq.at[whose], sqs.at[k - 1], sqr.at[k - 1], r, (s + k) % 4)
-
-    for k in (2, 3, 1):
-        share(k, s).start()
+    bytes_of(sq.at[0:31], sqr)
+    total = sq[0]
+    for j in range(1, 32):
+        total += sq[j]
+    sq_out[...] = total
     for j in range(6):
         to_core(j).wait_send()
-    for j in range(8):
+    for j in range(10):
         by_x(j).wait_send()
         by_y(j).wait_send()
         by_core(j, yy, was, war).wait_send()
@@ -420,22 +462,29 @@
     for m in range(3):
         stage1(G - 2, m).wait_send()
         stage1(G - 1, m).wait_send()
+    bytes_of(ryg, sys.at[0])
+    bytes_of(ryd, sys.at[1])
     bytes_of(r2g, s2s.at[0])
     bytes_of(r2d, s2s.at[1])
     bytes_of(gfin.at[:, :, 0 : 7 * 16, :], s3s)
     bytes_of(dfin.at[:, 0:304, :], s3ds)
-    for k in (1, 2, 3):
-        share(k, (s + 4 - k) % 4).wait()
-    sq_out[...] = ((sq[0] + sq[1]) + sq[2]) + sq[3]
+    bytes_of(sq.at[0:31], sqs)
     out_g.wait()
     out_d.wait()
 
 
-def adamw(w, m, v, g):
-    m = 0.9 * m + 0.1 * g
-    v = 0.95 * v + 0.05 * g * g
-    step = m * lax.rsqrt(v + 1e-8) + 0.1 * w
-    return (w - 0.02 * step).astype(BF), m, v
+def optimizer(sq_ref, *refs):
+    count = 4 * L * (2 * DS * FF + FS * D)
+    factor = jnp.minimum(1.0, 0.5 * lax.rsqrt(jnp.sum(sq_ref[...], keepdims=True) / count + 1e-30))
+    for i in range(3):
+        g, w, m, v = (refs[3 * which + i] for which in range(4))
+        g = g[...].reshape(w.shape).astype(F32) * factor.reshape(1, 1, 1)
+        new_m = 0.9 * m[...] + 0.1 * g
+        new_v = 0.95 * v[...] + 0.05 * g * g
+        step = new_m * lax.rsqrt(new_v + 1e-8) + 0.1 * w[...].astype(F32)
+        refs[12 + i][...] = (w[...].astype(F32) - 0.02 * step).astype(BF)
+        refs[15 + i][...] = new_m
+        refs[18 + i][...] = new_v
 
 
 def solution(mesh):
@@ -477,28 +526,41 @@
                 pltpu.VMEM((4, FC // 4, D), F32),
                 pltpu.VMEM((G, 2, DS, FC), BF),
                 pltpu.VMEM((G, FC // 4, D), BF),
-                pltpu.VMEM((G, 2, 7, 16, FC), BF),
-                pltpu.VMEM((G, 7, 16, 256), BF),
+                pltpu.VMEM((G, 2, DS // 2, FC), BF),
+                pltpu.VMEM((G, FC // 8, D), BF),
+                pltpu.VMEM((G, 2, 3, 16, FC), BF),
+                pltpu.VMEM((G, 3, 16, 256), BF),
                 pltpu.VMEM((G, 2, 16, FC), BF),
                 pltpu.VMEM((G, 16, 256), BF),
                 pltpu.VMEM((L, 2, DS, FF), BF),
                 pltpu.VMEM((L, FS, D), BF),
-                pltpu.VMEM((4, 8, 128), F32),
+                pltpu.VMEM((8, 128), F32),
+                pltpu.VMEM((32, 8, 128), F32),
                 dma((2,)),
                 dma((6,)), dma((6,)), dma((6,)),
-                dma((8,)), dma((8,)), dma((8,)), dma((8,)), dma((8,)), dma((8,)), dma((8,)), dma((8,)),
+                dma((10,)), dma((10,)), dma((10,)), dma((10,)), dma((10,)), dma((10,)), dma((10,)), dma((10,)),
                 dma((2, 2)), dma((2, 6)), dma((2, 3)), dma((G, 3)),
-                dma((2,)), dma((G, 21)),
+                dma((2,)), dma((G, 3)), dma((2,)), dma((G, 9)),
                 dma(()), dma(()), dma(()), dma(()),
-                dma((3,)), dma((3,)), dma((2,)),
+                dma(()), dma(()), dma((2,)),
             ],
             compiler_params=pltpu.CompilerParams(collective_id=0, has_side_effects=True, vmem_limit_bytes=67043328),
         )(x, dy, *weights)
-        count = 4 * (gu.size + d.size)
-        factor = jnp.minimum(1.0, 0.5 * lax.rsqrt(jnp.sum(sq) / count + 1e-30))
-        grads = (gu[:, 0], gu[:, 1], d)
-        new = [adamw(w.astype(F32), m, v, g.astype(F32) * factor) for w, m, v, g in zip(weights, ms, vs, grads, strict=True)]
-        return tuple(one[which] for which in range(3) for one in new)
+        wide = pl.BlockSpec((1, DS // STEPS, FF), lambda l, i: (l, i, 0))
+        deep = pl.BlockSpec((1, FS // STEPS, D), lambda l, i: (l, i, 0))
+        three = [wide, wide, deep]
+        gate = pl.BlockSpec((1, 1, DS // STEPS, FF), lambda l, i: (l, 0, i, 0))
+        up = pl.BlockSpec((1, 1, DS // STEPS, FF), lambda l, i: (l, 1, i, 0))
+        new = pl.pallas_call(
+            optimizer,
+            name="optimizer",
+            grid=(L, STEPS),
+            out_shape=[jax.ShapeDtypeStruct(a.shape, t) for t, which in ((BF, weights), (F32, ms), (F32, vs)) for a in which],
+            in_specs=[pl.BlockSpec((8, 128), lambda l, i: (0, 0)), gate, up, deep] + three * 3,
+            out_specs=three * 3,
+            compiler_params=pltpu.CompilerParams(dimension_semantics=("arbitrary", "arbitrary")),
+        )(sq, gu, gu, d, *weights, *ms, *vs)
+        return tuple(new)
 
     states, cut = P(("rep", "r", "s"), None, None), P(None, "s", None)
     return jax.shard_map(

time: 207 us -> 181 us (0.87)
  Pallas kernels: 195 us -> 180 us
  other arithmetic: 10.3 us -> 0 us
    pallas_call x1, Pallas kernels: 195 us -> 170 us  [step(): pl.pallas_call(kernel, name='train_step', out_shape=(jax.ShapeDtypeStruct...]
    pallas_call x0 -> x1, Pallas kernels: none -> 10.8 us  [step(): pl.pallas_call(optimizer, name='optimizer', grid=(L, STEPS), out_shape=[j...]
    convert_element_type x2 -> x0, other arithmetic: 8.99 us -> none  [adamw(): return ((w - 0.02 * step).astype(BF), m, v)]
where the time goes in v2:
time: 181 us
  Pallas kernels  180 us (99%)
    pallas_call x1, Pallas kernels, step(): pl.pallas_call(kernel, name='train_step', out_shape=(jax.ShapeDtypeStruct...  170 us
    pallas_call x1, Pallas kernels, step(): pl.pallas_call(optimizer, name='optimizer', grid=(L, STEPS), out_shape=[j...  10.8 us

profile of v2, /device:TPU:0, one launch (start us, length us, event | category | flops | bytes accessed | tf_op | source)
XLA Modules:
  0.0 181.1 jit_solution(8640022439548259659)
XLA Ops:
  0.6 169.6 %train_step.1 = (bf16[2,2,128,1280]{3,2,1,0:T(8,128)(2,1)}, bf16[2,320,512]{2,1,0:T(8,128)(2,1)}, f32[8,128]{1,0:T(8,128)}) custom-call(bf16[1,4096,512]{2,1,0:T(8,128)(2,1)} %x_in.1, bf16[1,4096,512]{2,1,0:T(8,128)(2,1)} %dy_in.1, bf16[2,128,1280]{2,1,0:T(8,128)(2,1)} %refs_3_.1, bf16[2,128,1280]{2,1,0:T(8,128)(2,1)} %refs_4_.1, bf16[2,320,512]{2,1,0:T(8,128)(2,1)} %refs_5_.1), custom_call_target="tpu_custom_call" | custom-call | tf_op jit(solution)/shard_map/train_step/pallas_call | solution.py:495
  170.3 10.8 %optimizer.1 = (bf16[2,128,1280]{2,1,0:T(8,128)(2,1)}, bf16[2,128,1280]{2,1,0:T(8,128)(2,1)}, bf16[2,320,512]{2,1,0:T(8,128)(2,1)}, f32[2,128,1280]{2,1,0:T(8,12...) custom-call(f32[8,128]{1,0:T(8,128)} %get-tuple-element.12.sq_ref, ...), custom_call_target="tpu_custom_call" | custom-call | tf_op jit(solution)/shard_map/optimizer/pallas_call | solution.py:554

commit v3 on v2

--- a/solution.py
+++ b/solution.py
@@ -1,5 +1,3 @@
-import functools
-
 import jax
 import jax.numpy as jnp
 from jax import lax
@@ -9,14 +7,16 @@
 
 MESH = pl.DeviceIdType.MESH
 BF, F32 = jnp.bfloat16, jnp.float32
+ALL, MATRICES, OTHERS, BOTH = slice(None), range(3), range(1, 32), (1, 0)
 T, D, FF, L = 4096, 512, 1280, 2
 TB, FC = 512, 256
 NT, NC = T // TB, FF // FC
 TBB, SB = 1024, 256
 BB = T // TBB
 G = L * NC
-STEPS = 4
+STEPS = 1
 DS, FS = D // 4, FF // 4
+QR, GU = FC // 4, (2, DS, FC)
 
 
 def dot(a, b):
@@ -39,14 +39,18 @@
     return pl.multiple_of(i * n, n)
 
 
-def kernel(x_in, dy_in, wg_in, wu_in, wd_in, gu_out, d_out, sq_out, *scratch):
-    (hb, dyb, a0, a1, a0t, a1t, dyt, da, wgu, wd, acc, sbg, sbd, r0g, r0d, t1g, t1d, r1g, r1d, o32g, o32d, s2g, s2d, ryg, ryd, r2g, r2d,
-     fg, fd, gfin, dfin, sqacc, sq, ld, wla, wcs, wcr, wxs, wxr, wys, wyr, was, war, wbs, wbr,
-     s0s, s0r, s1s, s1r, sys, syr, s2s, s2r, s3s, s3r, s3ds, s3dr, sqs, sqr, osem) = scratch
+def kernel(x_in, dy_in, wg_in, wu_in, wd_in, gu_out, d_out, sq_out, kept, *scratch):
+    (hb, dyb, a0, a1, at, dyt, da, wgu, wd, acc, sbg, sbd, r0g, r0d, t1g, t1d, r1g, r1d, o32g, o32d, s2g, s2d, ryg, ryd, r2g, r2d,
+     fg, fd, gfin, dfin, sqacc, sq, st, sts, ks, ld, wla, wcs, wcr, wxs, wxr, wys, wyr, was, war, wbs, wbr,
+     s0s, s0r, s1s, s1r, sys, syr, s2s, s2r, s3s, s3r, s3ys, s3yr, s3ds, s3dr, sqs, sqr, osem) = scratch
     s, r = lax.axis_index("s"), lax.axis_index("r")
     xx, cc, yy = s // 2, s % 2, r // 4
-    s1, s2, s3 = 2 * xx + 1 - cc, 2 * (1 - xx) + cc, 2 * (1 - xx) + 1 - cc
+    s1, s2 = s + 1 - 2 * cc, (s + 2) % 4
+    s3 = (s1 + 2) % 4
     across = (r + 4) % 8
+
+    def other(k):
+        return {"r": (r + k // 4) % 8, "s": (s + k) % 4}
 
     def remote(src, dst, send, recv, rr, ss):
         return pltpu.make_async_remote_copy(
@@ -54,10 +58,8 @@
         )
 
     barrier = pltpu.get_barrier_semaphore()
-    for dr in (0, 4, 1, 7, 5, 3, 2, 6):
-        for ds in range(4):
-            if (dr, ds) != (0, 0):
-                pl.semaphore_signal(barrier, inc=1, device_id={"r": (r + dr) % 8, "s": (s + ds) % 4}, device_id_type=MESH)
+    for k in OTHERS:
+        pl.semaphore_signal(barrier, inc=1, device_id=other(k), device_id_type=MESH)
 
     WIDE = (512, 768)
 
@@ -130,7 +132,6 @@
         wide = hb[rows, :].astype(F32)
         a = (wide * norm_scale(wide)).astype(BF)
         a0[rows, :] = a
-        a0t[:, rows] = a.T
         dyt[:, rows] = dyb[rows, :].T
 
         @pl.when(i == 6)
@@ -141,17 +142,32 @@
 
     lax.fori_loop(0, NT, prologue, 0)
 
-    def mlp(a, start, width):
+    def mlp(a, start, width, slot):
         o = None
         for c in range(width // FC):
             cols = pl.ds(pl.multiple_of(start + c * FC, FC), FC)
             g = dot(a, wgu[0, 0, :, cols])
             u = dot(a, wgu[0, 1, :, cols])
+            st[slot, c, :, :FC] = g
+            st[slot, c, :, FC:] = u
             p = (g * sigmoid(g) * u).astype(BF)
             one = dot(p, wd[0, cols, :])
             o = one if o is None else o + one
         return o
 
+    def keep(i, part):
+        slot, count = i % 2, WIDE[part] // FC
+        return pltpu.make_async_copy(
+            st.at[slot, :count],
+            kept.at[pl.ds(first(part, xx) // FC, count), pl.ds(aligned(i, TB), TB), :],
+            sts.at[slot],
+        )
+
+    def free_slot(i, part):
+        @pl.when(i >= 2)
+        def _():
+            keep(i, part).wait()
+
     def fwd_first(i, _):
         @pl.when(i == 2)
         def _():
@@ -161,15 +177,17 @@
         def _():
             got_x(4)
 
+        free_slot(i, 0)
         rows = pl.ds(aligned(i, TB), TB)
-        da[rows, :] = mlp(a0[rows, :], first(0, xx), WIDE[0])
+        da[rows, :] = mlp(a0[rows, :], first(0, xx), WIDE[0], i % 2)
+        keep(i, 0).start()
         return 0
 
     def fwd_second(i, _):
         @pl.when(i == 0)
         def _():
-            got_x(5)
-            got_x(6)
+            for j in (5, 6):
+                got_x(j)
 
         @pl.when(i == 1)
         def _():
@@ -189,31 +207,36 @@
             got_x(9)
             got_y(7)
 
+        free_slot(i, 1)
         rows = pl.ds(aligned(i, TB), TB)
-        o = da[rows, :] + mlp(a0[rows, :], first(1, xx), WIDE[1])
+        o = da[rows, :] + mlp(a0[rows, :], first(1, xx), WIDE[1], i % 2)
+        keep(i, 1).start()
         da[rows, :] = jnp.zeros((TB, D), F32)
         h = hb[rows, :] + o.astype(BF)
         hb[rows, :] = h
         wide = h.astype(F32)
         a = (wide * norm_scale(wide)).astype(BF)
         a1[rows, :] = a
-        a1t[:, rows] = a.T
+        at[:, rows] = a.T
         return 0
 
     got_x(1)
     got_y(0)
     got_y(1)
     got_x(2)
-    for j in range(3):
+    for j in MATRICES:
         to_core(j).wait_recv()
     got_core(0)
     got_core(1)
     lax.fori_loop(0, NT, fwd_first, 0)
-    for j in (2, 3, 4):
-        got_y(j)
-    for j in (2, 3, 4):
-        got_core(j)
+    keep(NT - 2, 0).wait()
+    keep(NT - 1, 0).wait()
+    for get in (got_y, got_core):
+        for j in (2, 3, 4):
+            get(j)
     lax.fori_loop(0, NT, fwd_second, 0)
+    keep(NT - 2, 1).wait()
+    keep(NT - 1, 1).wait()
     for j in range(3, 6):
         to_core(j).wait_recv()
     for j in (5, 6, 7):
@@ -227,7 +250,7 @@
 
     def stage0(g, m, w):
         slot = g % 2
-        src = mine(m, sbg, sbd)(slot, part(m, (s1, s3)[w]), slice(None))
+        src = mine(m, sbg, sbd)(slot, part(m, (s1, s3)[w]), ALL)
         return remote(src, mine(m, r0g, r0d)(slot, w), s0s.at[slot, m // 2], s0r.at[slot, 2 * m + w], r, s1)
 
     def stage0_sent(g):
@@ -236,19 +259,19 @@
         pltpu.make_async_copy(r0d.at[slot], r0d.at[slot], s0s.at[slot, 1]).wait()
 
     def stage1(g, m):
-        return remote(mine(m, t1g, t1d)(g % 2), mine(m, r1g, r1d)(g), s1s.at[g % 2, m], s1r.at[g, m], r, s2)
+        return remote(mine(m, t1g, t1d)(g), mine(m, r1g, r1d)(g), s1s.at[m // 2], s1r.at[g, m], r, s2)
 
     def piece(m, who):
         if m == 2:
             return pl.ds(aligned(who // 2, 16), 16), pl.ds(aligned(who % 2, 256), 256)
-        return pl.ds(aligned(who, 16), 16), slice(None)
+        return pl.ds(aligned(who, 16), 16), ALL
 
     def half(m, y):
         return pl.ds(aligned(y, 32), 32) if m == 2 else pl.ds(aligned(y, 64), 64)
 
     def stage2y(g, m):
         return remote(
-            mine(m, s2g, s2d)(g, half(m, 1 - yy), slice(None)), mine(m, ryg, ryd)(g), sys.at[m // 2], syr.at[g, m], across, s
+            mine(m, s2g, s2d)(g, half(m, 1 - yy), ALL), mine(m, ryg, ryd)(g), sys.at[m // 2], syr.at[g, m], across, s
         )
 
     def stage2(g, m, k):
@@ -263,24 +286,33 @@
         return 1 - g // NC, g % NC, block // 5, spot
 
     def stage3(g, m, k):
-        to = (r + k) % 8
         layer, c, owner, spot = place(g)
         if m == 2:
-            return remote(fd.at[g], dfin.at[(layer, *spot)], s3ds, s3dr, to, owner)
-        return remote(fg.at[g, m], gfin.at[layer, m, pl.ds(aligned(r, 16), 16), pl.ds(aligned(c, FC), FC)], s3s, s3r, to, s)
-
-    def add0(g, m, fresh):
+            return remote(fd.at[g], dfin.at[(layer, *spot)], s3ds, s3dr, (r + k) % 8, owner)
+        to = 4 * yy + (r % 4 + k) % 4
+        where = gfin.at[layer, m, pl.ds(aligned(r, 16), 16), pl.ds(aligned(c, FC), FC)]
+        return remote(fg.at[g, m], where, s3s, s3r.at[g, m], to, s)
+
+    def stage3y(g, m):
+        layer, c, _, _ = place(g)
+        block = gfin.at[layer, m, pl.ds(aligned(yy, 64), 64), pl.ds(aligned(c, FC), FC)]
+        return remote(block, block, s3ys, s3yr, across, s)
+
+    def add3(g, m):
+        if m < 2:
+            pltpu.make_async_copy(r2g.at[g, m], r2g.at[g, m], s3r.at[g, m]).wait()
+            stage3y(g, m).start()
+
+    def add0(g, m):
         slot = g % 2
-        for w in (1, 0):
+        for w in BOTH:
             stage0(g, m, w).wait_recv()
-        if not fresh:
-            stage1(g, m).wait_send()
         own_term = mine(m, sbg, sbd)
         arrived = mine(m, r0g, r0d)
-        other = own_term(slot, part(m, s2), slice(None))[...].astype(F32) + arrived(slot, 1)[...].astype(F32)
-        mine(m, t1g, t1d)(slot)[...] = other.astype(BF)
+        other = own_term(slot, part(m, s2), ALL)[...].astype(F32) + arrived(slot, 1)[...].astype(F32)
+        mine(m, t1g, t1d)(g)[...] = other.astype(BF)
         stage1(g, m).start()
-        kept = own_term(slot, part(m, s), slice(None))[...].astype(F32) + arrived(slot, 0)[...].astype(F32)
+        kept = own_term(slot, part(m, s), ALL)[...].astype(F32) + arrived(slot, 0)[...].astype(F32)
         mine(m, o32g, o32d)(g % 4)[...] = kept
 
     def add1(g, m):
@@ -292,24 +324,24 @@
 
     def add2y(g, m):
         stage2y(g, m).wait_recv()
-        here = half(m, yy), slice(None)
+        here = half(m, yy), ALL
         total = mine(m, o32g, o32d)(g % 4, *here)[...] + mine(m, ryg, ryd)(g)[...].astype(F32)
         mine(m, o32g, o32d)(g % 4, *here)[...] = total
         mine(m, s2g, s2d)(g, *here)[...] = total.astype(BF)
-        for k in (2, 3, 1):
+        for k in range(3, 0, -1):
             stage2(g, m, k).start()
 
     def add2(g, m):
         for k in range(1, 4):
             stage2(g, m, k).wait_recv()
         total = mine(m, o32g, o32d)(g % 4, *piece(m, r))[...]
-        for k in range(3):
+        for k in MATRICES:
             total += mine(m, r2g, r2d)(g, k)[...].astype(F32)
         total = total.astype(BF)
         mine(m, fg, fd)(g)[...] = total
         square = total.astype(F32)
         square = square * square
-        sqacc[...] += (square[:8, :128] + square[:8, 128:]) + (square[8:, :128] + square[8:, 128:])
+        sqacc[...] += square[:8, :128] + square[:8, 128:] + square[8:, :128] + square[8:, 128:]
         layer, c, owner, spot = place(g)
         if m == 2:
 
@@ -322,10 +354,14 @@
                 stage3(g, m, 0).start()
         else:
             gfin[layer, m, pl.ds(aligned(r, 16), 16), pl.ds(aligned(c, FC), FC)] = total
-        for k in (4, 5, 3, 6, 2, 7, 1):
+        for k in range(7 if m == 2 else 3, 0, -1):
             stage3(g, m, k).start()
 
-    def backward(layer, a_ref, at_ref, with_da):
+    def recall(c, at_row, count):
+        rows = pl.ds(pl.multiple_of(at_row, TB), count)
+        return pltpu.make_async_copy(kept.at[c, rows, :], da.at[rows, :], ks.at[at_row // TBB])
+
+    def backward(layer, with_da):
         def chunk(c, _):
             cols = pl.ds(aligned(c, FC), FC)
             n = (1 - layer) * NC + c
@@ -333,23 +369,27 @@
             def block(i, _):
                 @pl.when((i == 0) & (n >= 2))
                 def _():
-                    for m in range(3):
+                    for m in MATRICES:
                         add1(n - 2, m)
 
-                @pl.when((i == 1) & (n >= 3))
+                @pl.when((i == 1) & (n >= 4))
                 def _():
-                    for m in range(3):
-                        add0(n - 1, m, False)
+                    for m in range(2):
+                        add3(n - 4, m)
+
+                @pl.when((i == 1) & (n >= 1))
+                def _():
+                    for m in MATRICES:
+                        add0(n - 1, m)
+
+                @pl.when((i == 2) & (n >= 3))
+                def _():
+                    for m in MATRICES:
                         add2(n - 3, m)
 
-                @pl.when((i == 1) & (n >= 1) & (n < 3))
+                @pl.when((i == 3) & (n >= 2))
                 def _():
-                    for m in range(3):
-                        add0(n - 1, m, True)
-
-                @pl.when((i == 2) & (n >= 2))
-                def _():
-                    for m in range(3):
+                    for m in MATRICES:
                         add2y(n - 2, m)
 
                 if with_da:
@@ -367,13 +407,19 @@
                         got_core(8)
                         got_core(9)
 
+                if not with_da:
+                    recall(c, i * TBB, TBB).wait()
+
                 def rows(q):
                     return pl.ds(aligned(i * (TBB // SB) + q, SB), SB)
 
                 def front(q):
-                    a = a_ref[rows(q), :]
-                    g = dot(a, wgu[layer, 0, :, cols])
-                    u = dot(a, wgu[layer, 1, :, cols])
+                    if with_da:
+                        a = a1[rows(q), :]
+                        g = dot(a, wgu[layer, 0, :, cols])
+                        u = dot(a, wgu[layer, 1, :, cols])
+                    else:
+                        g, u = da[rows(q), :FC], da[rows(q), FC:]
                     dp = dot_t(dyb[rows(q), :], wd[layer, cols, :]).astype(BF).astype(F32)
                     sig = sigmoid(g)
                     sl = g * sig
@@ -381,15 +427,26 @@
                     return (dp * u * dsl).astype(BF), (dp * sl).astype(BF), (sl * u).astype(BF)
 
                 def back(qs, of):
-                    for m, left in enumerate((at_ref, at_ref, dyt)):
+                    for m, left in enumerate((at, at, dyt)):
                         base = jnp.where(i > 0, acc[m], 0.0) if qs[0] == 0 else acc[m]
                         acc[m] = base + sum(dot(left[:, rows(q)], of[q][m]) for q in qs)
                     if with_da:
                         for q in qs:
                             da[rows(q), :] += dot_t(of[q][0], wgu[layer, 0, :, cols]) + dot_t(of[q][1], wgu[layer, 1, :, cols])
 
-                of = [front(q) for q in range(4)]
-                back((0, 1, 2, 3), of)
+                if with_da:
+                    of = [front(q) for q in range(4)]
+                    back((0, 1, 2, 3), of)
+                else:
+                    of = [front(q) for q in range(4)]
+                    back((0, 1), of)
+                    back((2, 3), of)
+                if not with_da:
+
+                    @pl.when(c < NC - 1)
+                    def _():
+                        recall(c + 1, i * TBB, TBB).start()
+
                 return 0
 
             lax.fori_loop(0, BB, block, 0)
@@ -399,15 +456,15 @@
             def _():
                 stage0_sent(n)
 
-            for m in range(3):
+            for m in MATRICES:
                 mine(m, sbg, sbd)(slot)[...] = (acc[m].T if m == 2 else acc[m]).astype(BF)
-                for w in (1, 0):
+                for w in BOTH:
                     stage0(n, m, w).start()
             return 0
 
         lax.fori_loop(0, NC, chunk, 0)
 
-    backward(1, a1, a1t, True)
+    backward(1, True)
 
     def norm_back(i, _):
         rows = pl.ds(aligned(i, TB), TB)
@@ -418,34 +475,37 @@
         dh = dyb[rows, :] + back.astype(BF)
         dyb[rows, :] = dh
         dyt[:, rows] = dh.T
+        at[:, rows] = a0[rows, :].T
+        recall(0, i * TB, TB).start()
         return 0
 
     lax.fori_loop(0, NT, norm_back, 0)
-    backward(0, a0, a0t, False)
-
-    for which, g in ((add1, G - 2), (add2, G - 3), (functools.partial(add0, fresh=False), G - 1), (add2y, G - 2), (add1, G - 1),
-                     (add2, G - 2), (add2y, G - 1), (add2, G - 1)):
-        for m in range(3):
+    backward(0, False)
+
+    for which, g in ((add1, G - 2), (add3, G - 4), (add2, G - 3), (add0, G - 1), (add2y, G - 2), (add1, G - 1), (add3, G - 3),
+                     (add2y, G - 1), (add2, G - 2), (add2, G - 1)):
+        for m in MATRICES:
             which(g, m)
 
     me = 4 * r + s
     sq[me] = sqacc[...]
-    for dr in range(8):
-        for ds in range(4):
-            if (dr, ds) != (0, 0):
-                remote(sq.at[me], sq.at[me], sqs, sqr, (r + dr) % 8, (s + ds) % 4).start()
+    for k in OTHERS:
+        remote(sq.at[me], sq.at[me], sqs, sqr, *other(k).values()).start()
 
     def bytes_of(ref, sem):
         pltpu.make_async_copy(ref, ref, sem).wait()
 
-    bytes_of(gfin.at[:, :, 0 : 7 * 16, :], s3r)
-    bytes_of(dfin.at[:, 0:304, :], s3dr)
+    for g in (G - 2, G - 1):
+        for m in range(2):
+            add3(g, m)
+    bytes_of(gfin.at[:, :, :64], s3yr)
+    bytes_of(dfin.at[:, :304], s3dr)
     out_g = pltpu.make_async_copy(gfin, gu_out, osem.at[0])
     out_d = pltpu.make_async_copy(dfin, d_out, osem.at[1])
     out_g.start()
     out_d.start()
 
-    bytes_of(sq.at[0:31], sqr)
+    bytes_of(sq.at[:31], sqr)
     total = sq[0]
     for j in range(1, 32):
         total += sq[j]
@@ -459,16 +519,16 @@
         by_core(j, 1 - yy, wbs, wbr).wait_send()
     stage0_sent(G - 2)
     stage0_sent(G - 1)
-    for m in range(3):
-        stage1(G - 2, m).wait_send()
-        stage1(G - 1, m).wait_send()
+    bytes_of(t1g, s1s.at[0])
+    bytes_of(t1d, s1s.at[1])
     bytes_of(ryg, sys.at[0])
     bytes_of(ryd, sys.at[1])
     bytes_of(r2g, s2s.at[0])
     bytes_of(r2d, s2s.at[1])
-    bytes_of(gfin.at[:, :, 0 : 7 * 16, :], s3s)
-    bytes_of(dfin.at[:, 0:304, :], s3ds)
-    bytes_of(sq.at[0:31], sqs)
+    bytes_of(r2g, s3s)
+    bytes_of(gfin.at[:, :, :64], s3ys)
+    bytes_of(dfin.at[:, :304], s3ds)
+    bytes_of(sq.at[:31], sqs)
     out_g.wait()
     out_d.wait()
 
@@ -476,7 +536,7 @@
 def optimizer(sq_ref, *refs):
     count = 4 * L * (2 * DS * FF + FS * D)
     factor = jnp.minimum(1.0, 0.5 * lax.rsqrt(jnp.sum(sq_ref[...], keepdims=True) / count + 1e-30))
-    for i in range(3):
+    for i in MATRICES:
         g, w, m, v = (refs[3 * which + i] for which in range(4))
         g = g[...].reshape(w.shape).astype(F32) * factor.reshape(1, 1, 1)
         new_m = 0.9 * m[...] + 0.1 * g
@@ -492,22 +552,22 @@
         weights, ms, vs = (arrays[i : i + 3] for i in (0, 3, 6))
         hbm = pl.BlockSpec(memory_space=pl.ANY)
         dma = pltpu.SemaphoreType.DMA
-        gu, d, sq = pl.pallas_call(
+        gu, d, sq, _ = pl.pallas_call(
             kernel,
             name="train_step",
             out_shape=(
                 jax.ShapeDtypeStruct((L, 2, DS, FF), BF),
                 jax.ShapeDtypeStruct((L, FS, D), BF),
                 jax.ShapeDtypeStruct((8, 128), F32),
+                jax.ShapeDtypeStruct((NC, T, 2 * FC), F32),
             ),
             in_specs=[hbm] * 5,
-            out_specs=(hbm, hbm, pl.BlockSpec(memory_space=pltpu.VMEM)),
+            out_specs=(hbm, hbm, pl.BlockSpec(memory_space=pltpu.VMEM), hbm),
             scratch_shapes=[
                 pltpu.VMEM((T, D), BF),
                 pltpu.VMEM((T, D), BF),
                 pltpu.VMEM((T, D), BF),
                 pltpu.VMEM((T, D), BF),
-                pltpu.VMEM((D, T), BF),
                 pltpu.VMEM((D, T), BF),
                 pltpu.VMEM((D, T), BF),
                 pltpu.VMEM((T, D), F32),
@@ -517,15 +577,15 @@
                 pltpu.VMEM((2, 2, D, FC), BF),
                 pltpu.VMEM((2, FC, D), BF),
                 pltpu.VMEM((2, 2, 2, DS, FC), BF),
-                pltpu.VMEM((2, 2, FC // 4, D), BF),
-                pltpu.VMEM((2, 2, DS, FC), BF),
-                pltpu.VMEM((2, FC // 4, D), BF),
-                pltpu.VMEM((G, 2, DS, FC), BF),
-                pltpu.VMEM((G, FC // 4, D), BF),
-                pltpu.VMEM((4, 2, DS, FC), F32),
-                pltpu.VMEM((4, FC // 4, D), F32),
-                pltpu.VMEM((G, 2, DS, FC), BF),
-                pltpu.VMEM((G, FC // 4, D), BF),
+                pltpu.VMEM((2, 2, QR, D), BF),
+                pltpu.VMEM((G, *GU), BF),
+                pltpu.VMEM((G, QR, D), BF),
+                pltpu.VMEM((G, *GU), BF),
+                pltpu.VMEM((G, QR, D), BF),
+                pltpu.VMEM((4, *GU), F32),
+                pltpu.VMEM((4, QR, D), F32),
+                pltpu.VMEM((G, *GU), BF),
+                pltpu.VMEM((G, QR, D), BF),
                 pltpu.VMEM((G, 2, DS // 2, FC), BF),
                 pltpu.VMEM((G, FC // 8, D), BF),
                 pltpu.VMEM((G, 2, 3, 16, FC), BF),
@@ -536,13 +596,14 @@
                 pltpu.VMEM((L, FS, D), BF),
                 pltpu.VMEM((8, 128), F32),
                 pltpu.VMEM((32, 8, 128), F32),
+                pltpu.VMEM((2, 3, TB, 2 * FC), F32),
+                dma((2,)), dma((BB,)),
                 dma((2,)),
-                dma((6,)), dma((6,)), dma((6,)),
-                dma((10,)), dma((10,)), dma((10,)), dma((10,)), dma((10,)), dma((10,)), dma((10,)), dma((10,)),
-                dma((2, 2)), dma((2, 6)), dma((2, 3)), dma((G, 3)),
+                *[dma((6,))] * 3,
+                *[dma((10,))] * 8,
+                dma((2, 2)), dma((2, 6)), dma((2,)), dma((G, 3)),
                 dma((2,)), dma((G, 3)), dma((2,)), dma((G, 9)),
-                dma(()), dma(()), dma(()), dma(()),
-                dma(()), dma(()), dma((2,)),
+                dma(()), dma((G, 2)), *[dma(())] * 6, dma((2,)),
             ],
             compiler_params=pltpu.CompilerParams(collective_id=0, has_side_effects=True, vmem_limit_bytes=67043328),
         )(x, dy, *weights)
@@ -562,7 +623,7 @@
         )(sq, gu, gu, d, *weights, *ms, *vs)
         return tuple(new)
 
-    states, cut = P(("rep", "r", "s"), None, None), P(None, "s", None)
+    states, cut = P(("rep", "r", "s")), P(None, "s")
     return jax.shard_map(
-        step, mesh=mesh, in_specs=(states, states) + (cut,) * 9, out_specs=(P("rep", "s", None),) * 9, check_vma=False
+        step, mesh=mesh, in_specs=(states, states) + (cut,) * 9, out_specs=(P("rep", "s"),) * 9, check_vma=False
     )

time: 181 us -> 177 us (0.978)
  Pallas kernels: 180 us -> 176 us
    pallas_call x1, Pallas kernels: 10.8 us -> 8.73 us  [step(): pl.pallas_call(optimizer, name='optimizer', grid=(L, STEPS), out_shape=[j...]
    pallas_call x1, Pallas kernels: 170 us -> 168 us  [step(): pl.pallas_call(kernel, name='train_step', out_shape=(jax.ShapeDtypeStruct...]
where the time goes in v3:
time: 177 us
  Pallas kernels  176 us (99%)
    pallas_call x1, Pallas kernels, step(): pl.pallas_call(kernel, name='train_step', out_shape=(jax.ShapeDtypeStruct...  168 us
    pallas_call x1, Pallas kernels, step(): pl.pallas_call(optimizer, name='optimizer', grid=(L, STEPS), out_shape=[j...  8.73 us

profile of v3, /device:TPU:0, one launch (start us, length us, event | category | flops | bytes accessed | tf_op | source)
XLA Modules:
  0.0 177.1 jit_solution(9717825449561696642)
XLA Ops:
  0.6 167.6 %train_step.1 = (bf16[2,2,128,1280]{3,2,1,0:T(8,128)(2,1)}, bf16[2,320,512]{2,1,0:T(8,128)(2,1)}, f32[8,128]{1,0:T(8,128)}, f32[5,4096,512]{2,1,0:T(8,128)}) custom-call(bf16[1,4096,512]{2,1,0:T(8,128)(2,1)} %x_in.1, bf16[1,4096,512]{2,1,0:T(8,128)(2,1)} %dy_in.1, bf16[2,128,1280]{2,1,0:T(8,128)(2,1)} %refs_3_.1, bf16[2,128,1280]{2,1,0:T(8,128)(2,1)} %refs_4_.1, ...), custom_call_target="tpu_custom_call" | custom-call | tf_op jit(solution)/shard_map/train_step/pallas_call | solution.py:555
  168.2 8.7 %optimizer.1 = (bf16[2,128,1280]{2,1,0:T(8,128)(2,1)}, bf16[2,128,1280]{2,1,0:T(8,128)(2,1)}, bf16[2,320,512]{2,1,0:T(8,128)(2,1)}, f32[2,128,1280]{2,1,0:T(8,12...) custom-call(f32[8,128]{1,0:T(8,128)} %get-tuple-element.12.sq_ref, ...), custom_call_target="tpu_custom_call" | custom-call | tf_op jit(solution)/shard_map/optimizer/pallas_call | solution.py:615

commit v4 on v3

--- a/solution.py
+++ b/solution.py
@@ -134,9 +134,13 @@
         a0[rows, :] = a
         dyt[:, rows] = dyb[rows, :].T
 
-        @pl.when(i == 6)
+        @pl.when(i == 5)
         def _():
             got_x(0)
+
+        @pl.when(i == 7)
+        def _():
+            got_x(1)
 
         return 0
 
@@ -220,7 +224,6 @@
         at[:, rows] = a.T
         return 0
 
-    got_x(1)
     got_y(0)
     got_y(1)
     got_x(2)
@@ -328,7 +331,7 @@
         total = mine(m, o32g, o32d)(g % 4, *here)[...] + mine(m, ryg, ryd)(g)[...].astype(F32)
         mine(m, o32g, o32d)(g % 4, *here)[...] = total
         mine(m, s2g, s2d)(g, *here)[...] = total.astype(BF)
-        for k in range(3, 0, -1):
+        for k in (2, 3, 1):
             stage2(g, m, k).start()
 
     def add2(g, m):
@@ -354,7 +357,7 @@
                 stage3(g, m, 0).start()
         else:
             gfin[layer, m, pl.ds(aligned(r, 16), 16), pl.ds(aligned(c, FC), FC)] = total
-        for k in range(7 if m == 2 else 3, 0, -1):
+        for k in (4, 5, 3, 6, 2, 7, 1) if m == 2 else (2, 3, 1):
             stage3(g, m, k).start()
 
     def recall(c, at_row, count):
@@ -434,13 +437,9 @@
                         for q in qs:
                             da[rows(q), :] += dot_t(of[q][0], wgu[layer, 0, :, cols]) + dot_t(of[q][1], wgu[layer, 1, :, cols])
 
-                if with_da:
-                    of = [front(q) for q in range(4)]
-                    back((0, 1, 2, 3), of)
-                else:
-                    of = [front(q) for q in range(4)]
-                    back((0, 1), of)
-                    back((2, 3), of)
+                of = [front(q) for q in range(4)]
+                back((0, 1), of)
+                back((2, 3), of)
                 if not with_da:
 
                     @pl.when(c < NC - 1)
@@ -482,8 +481,8 @@
     lax.fori_loop(0, NT, norm_back, 0)
     backward(0, False)
 
-    for which, g in ((add1, G - 2), (add3, G - 4), (add2, G - 3), (add0, G - 1), (add2y, G - 2), (add1, G - 1), (add3, G - 3),
-                     (add2y, G - 1), (add2, G - 2), (add2, G - 1)):
+    for which, g in ((add1, G - 2), (add2, G - 3), (add0, G - 1), (add2y, G - 2), (add3, G - 4), (add1, G - 1), (add2y, G - 1),
+                     (add2, G - 2), (add3, G - 3), (add2, G - 1)):
         for m in MATRICES:
             which(g, m)
 

time: 177 us -> 176 us (level)
  no operation moved by 1% of the time
where the time goes in v4:
time: 176 us; the launch traced here: 175 us
  Pallas kernels  175 us (99%)
    pallas_call x1, Pallas kernels, step(): pl.pallas_call(kernel, name='train_step', out_shape=(jax.ShapeDtypeStruct...  166 us
    pallas_call x1, Pallas kernels, step(): pl.pallas_call(optimizer, name='optimizer', grid=(L, STEPS), out_shape=[j...  8.73 us

profile of v4, /device:TPU:0, one launch (start us, length us, event | category | flops | bytes accessed | tf_op | source)
XLA Modules:
  0.0 175.4 jit_solution(15250386051124806483)
XLA Ops:
  0.6 165.9 %train_step.1 = (bf16[2,2,128,1280]{3,2,1,0:T(8,128)(2,1)}, bf16[2,320,512]{2,1,0:T(8,128)(2,1)}, f32[8,128]{1,0:T(8,128)}, f32[5,4096,512]{2,1,0:T(8,128)}) custom-call(bf16[1,4096,512]{2,1,0:T(8,128)(2,1)} %x_in.1, bf16[1,4096,512]{2,1,0:T(8,128)(2,1)} %dy_in.1, bf16[2,128,1280]{2,1,0:T(8,128)(2,1)} %refs_3_.1, bf16[2,128,1280]{2,1,0:T(8,128)(2,1)} %refs_4_.1, ...), custom_call_target="tpu_custom_call" | custom-call | tf_op jit(solution)/shard_map/train_step/pallas_call | solution.py:554
  166.5 8.7 %optimizer.1 = (bf16[2,128,1280]{2,1,0:T(8,128)(2,1)}, bf16[2,128,1280]{2,1,0:T(8,128)(2,1)}, bf16[2,320,512]{2,1,0:T(8,128)(2,1)}, f32[2,128,1280]{2,1,0:T(8,12...) custom-call(f32[8,128]{1,0:T(8,128)} %get-tuple-element.12.sq_ref, ...), custom_call_target="tpu_custom_call" | custom-call | tf_op jit(solution)/shard_map/optimizer/pallas_call | solution.py:614
